TPU v7x, 32 devices: a whole 2x2x4 slice. The times are simulated.
32 devices in a mesh: slab: 8 (over y, x, core), tile: 4 (over z).
Axes of the slice: x: 2, y: 2, z: 4, core: 2. Of those that a mesh axis runs over, the one named last changes fastest.
Arguments:
- volume: float32 [128, 256, 1024], P('slab', 'tile'), may hold values from -0.3 to 0.3
- shears: float32 [8], replicated, may hold values from -0.4 to 0.4
- tile_shift: int32 [8, 4], P(None, 'tile'), may hold values from -1 to 1
- illumination: float32 [2, 128, 128], replicated, may hold values from -6 to 6
- measured: bfloat16 [1024, 128, 128], P(('slab', 'tile')), may hold values from 0.049804688 to 2.5
- frame_owner: int32 [1024, 1], P(('slab', 'tile')), may hold values from 0 to 7; in each aligned block of 32 rows (0 to 31, 32 to 63, ...) at most 8 rows name the same one
- frame_shift: int32 [1024], P(('slab', 'tile')), may hold values from -32 to 160
Outputs:
- volume_grad: float32 [128, 256, 1024], P('slab', 'tile')
Inputs may be any that keep to these rules, and one draw needn't show every extreme that they name: `frame_owner`: the 32 frames of one device name each angle at most 8 times, a bound that some block reaches.
All inputs are finite; a program needn't handle non-finite values.
Results may differ from a plain program's by a relative error of at most 0.012.
Values may be sent and summed in bfloat16 or wider, within the bound.
A program may use at most 256 MiB of HBM per device.

v0:
```python
import functools
import math

import jax
import jax.numpy as jnp
from jax import lax
from jax.experimental import pallas as pl
from jax.experimental.pallas import tpu as pltpu
from jax.sharding import PartitionSpec as P

LANES = 128
HALF = LANES // 2
HALO = 32
SMOOTHING = 0.25
WIRE = jnp.bfloat16
F32 = jnp.float32
BF16 = jnp.bfloat16
MESH = pl.DeviceIdType.MESH
ROOT = math.sqrt(0.5 * math.log2(math.e))
GROUP = 8
SIN_POLY = (3.1415926401307073, -5.1677100835078775, 2.550077523214199, -0.5982912856179897, 0.07765766030124945)
COS_POLY = (0.9999999532476078, -4.934792830619626, 4.0584113528622625, -1.331876568078962, 0.2196896110945085)


def lane_ids(shape):
    return lax.broadcasted_iota(jnp.int32, shape, len(shape) - 1)


def row_ids(shape):
    return lax.broadcasted_iota(jnp.int32, shape, len(shape) - 2)


def halo_join(low, high):
    lanes = lane_ids(low.shape)
    outer = (lanes < HALO) | (lanes >= LANES - HALO)
    return jnp.where(outer, low, pltpu.roll(high, HALF, 1))


def project_kernel(tiles, slices, beams, blocks, shears_ref, shift_ref, v_ref, out_ref, lhs, ker, res, comb):
    angles = shears_ref.shape[0]
    pairs = angles // 2
    own = blocks // tiles
    groups = beams // 8
    half_rows = slices * blocks

    def arrange(group, carried):
        for pair in range(4):
            col = pl.multiple_of((group * 4 + pair) * LANES, LANES)
            for duo in range(slices // 2):
                lower, upper = [], []
                for s in (2 * duo, 2 * duo + 1):
                    start = (s * groups + group) * (blocks * 8) + 2 * pair
                    first = v_ref[pl.ds(start, blocks, stride=8), :]
                    second = v_ref[pl.ds(start + 1, blocks, stride=8), :]
                    left = lane_ids(first.shape) < HALF
                    crossed = pltpu.roll(jnp.where(left, second, first), HALF, 1)
                    lower.append(jnp.where(left, first, crossed))
                    upper.append(jnp.where(left, crossed, second))
                row = 2 * duo * blocks
                lhs[row : row + 2 * blocks, pl.ds(col, LANES)] = jnp.concatenate(lower, 0).astype(BF16)
                row += half_rows
                lhs[row : row + 2 * blocks, pl.ds(col, LANES)] = jnp.concatenate(upper, 0).astype(BF16)
        return carried

    lax.fori_loop(0, groups, arrange, 0)
    shape = (HALF, LANES)
    base = (lane_ids(shape) - row_ids(shape) - HALO).astype(F32) * ROOT
    lanes = lane_ids((half_rows, LANES))
    lanes_s = lane_ids((slices, LANES))

    for p in range(pairs):
        steps = [shears_ref[p] * ROOT, shears_ref[p + pairs] * ROOT]

        def beam(q, carried):
            place = q.astype(F32) - (beams - 1) * 0.5
            row = pl.multiple_of(q * HALF, HALF)
            for side in range(2):
                gap = base - place * steps[side]
                ker[pl.ds(row, HALF), side * LANES : (side + 1) * LANES] = jnp.exp2(-(gap * gap)).astype(BF16)
            return carried

        lax.fori_loop(0, beams, beam, 0, unroll=8)
        res[...] = jnp.dot(lhs[...], ker[...], preferred_element_type=F32)
        sums = []
        for side in range(2):
            cols = slice(side * LANES, (side + 1) * LANES)
            near = pltpu.roll(res[0:half_rows, cols], HALO, 1)
            far = pltpu.roll(res[half_rows : 2 * half_rows, cols], HALO + HALF, 1)
            comb[0] = jnp.where(lanes >= HALO, near, 0.0) + jnp.where(lanes >= HALO + HALF, far, 0.0)
            comb[1] = jnp.where(lanes < HALO, near, 0.0) + jnp.where(lanes < HALO + HALF, far, 0.0)
            shift = shift_ref[p + side * pairs, 0]
            row_of = []
            for k in range(blocks):
                total = jnp.zeros((slices, LANES), F32)
                for o in range(2):
                    i = k - shift - o
                    inside = (i >= 0) & (i < blocks)
                    picked = comb[o, pl.ds(jnp.clip(i, 0, blocks - 1), slices, stride=blocks), :]
                    total += jnp.where(inside, picked, 0.0)
                row_of.append(total)
            sums.append(row_of)
        zero = jnp.zeros((slices, LANES), F32)
        for t in range(tiles):
            margins = []
            for side in range(2):
                for b in range(own):
                    out_ref[t, p, side * own + b] = sums[side][t * own + b].astype(WIRE)
                after = sums[side][(t + 1) * own] if t + 1 < tiles else zero
                before = sums[side][t * own - 1] if t > 0 else zero
                margins.append(jnp.where(lanes_s < HALF, after, before))
            out_ref[t, p, 2 * own] = halo_join(margins[0], margins[1]).astype(WIRE)


def project(shears, tile_shift, volume, tiles):
    slices, beams, width = volume.shape
    blocks = width // LANES
    angles = shears.shape[0]
    own = blocks // tiles
    view = volume.reshape(slices, beams // 8, 8, blocks, LANES).transpose(0, 1, 3, 2, 4).reshape(-1, LANES)
    rows = 2 * slices * blocks
    return pl.pallas_call(
        functools.partial(project_kernel, tiles, slices, beams, blocks),
        out_shape=jax.ShapeDtypeStruct((tiles, angles // 2, 2 * own + 1, slices, LANES), WIRE),
        in_specs=[
            pl.BlockSpec(memory_space=pltpu.SMEM),
            pl.BlockSpec(memory_space=pltpu.SMEM),
            pl.BlockSpec(memory_space=pltpu.VMEM),
        ],
        out_specs=pl.BlockSpec(memory_space=pltpu.VMEM),
        scratch_shapes=[
            pltpu.VMEM((rows, beams * HALF), BF16),
            pltpu.VMEM((beams * HALF, 2 * LANES), BF16),
            pltpu.VMEM((rows, 2 * LANES), F32),
            pltpu.VMEM((2, rows // 2, LANES), F32),
        ],
        compiler_params=pltpu.CompilerParams(vmem_limit_bytes=40 * 1024 * 1024),
        name="project",
    )(shears, tile_shift, view)


def greet(axes):
    barrier = pltpu.get_barrier_semaphore()
    total = 0
    for axis, count in axes:
        me = lax.axis_index(axis)
        for step in range(1, count):
            pl.semaphore_signal(
                barrier, inc=1, device_id={axis: lax.rem(me + step, count)}, device_id_type=MESH
            )
            total += 1
    pl.semaphore_wait(barrier, total)


def phase_exchange_kernel(tiles, slabs, part_ref, phase_ref, came, tile_send, tile_recv, slab_send, slab_recv):
    pairs = part_ref.shape[1]
    slices = part_ref.shape[3]
    me_t = lax.axis_index("tile")
    me_s = lax.axis_index("slab")
    greet((("tile", tiles), ("slab", slabs)))
    rows = pl.ds(pl.multiple_of(me_s * slices, slices), slices)

    def tile_copy(p, step):
        peer = lax.rem(me_t + step, tiles)
        return pltpu.make_async_remote_copy(
            src_ref=part_ref.at[peer, p],
            dst_ref=came.at[step - 1, p],
            send_sem=tile_send.at[step - 1, p],
            recv_sem=tile_recv.at[step - 1, p],
            device_id={"tile": peer},
            device_id_type=MESH,
        )

    def slab_copy(p, step):
        return pltpu.make_async_remote_copy(
            src_ref=phase_ref.at[p, :, rows, :],
            dst_ref=phase_ref.at[p, :, rows, :],
            send_sem=slab_send.at[step - 1, p],
            recv_sem=slab_recv.at[step - 1, p],
            device_id={"slab": lax.rem(me_s + step, slabs)},
            device_id_type=MESH,
        )

    for p in range(pairs):
        for step in range(1, tiles):
            tile_copy(p, step).start()
    for p in range(pairs):
        total = part_ref[me_t, p].astype(F32)
        for step in range(1, tiles):
            tile_copy(p, step).wait_recv()
            total += came[step - 1, p].astype(F32)
        phase_ref[p, :, rows, :] = total.astype(WIRE)
        for step in range(1, slabs):
            slab_copy(p, step).start()
    for p in range(pairs):
        for step in range(1, slabs):
            slab_copy(p, step).wait_recv()
    for p in range(pairs):
        for step in range(1, tiles):
            tile_copy(p, step).wait_send()
        for step in range(1, slabs):
            slab_copy(p, step).wait_send()


def phase_exchange(parts, tiles, slabs):
    pairs, pieces, slices = parts.shape[1:4]
    return pl.pallas_call(
        functools.partial(phase_exchange_kernel, tiles, slabs),
        out_shape=jax.ShapeDtypeStruct((pairs, pieces, slabs * slices, LANES), WIRE),
        in_specs=[pl.BlockSpec(memory_space=pltpu.VMEM)],
        out_specs=pl.BlockSpec(memory_space=pltpu.VMEM),
        scratch_shapes=[
            pltpu.VMEM((tiles - 1, pairs, pieces, slices, LANES), WIRE),
            pltpu.SemaphoreType.DMA((tiles - 1, pairs)),
            pltpu.SemaphoreType.DMA((tiles - 1, pairs)),
            pltpu.SemaphoreType.DMA((slabs - 1, pairs)),
            pltpu.SemaphoreType.DMA((slabs - 1, pairs)),
        ],
        compiler_params=pltpu.CompilerParams(
            collective_id=0, has_side_effects=True, vmem_limit_bytes=16 * 1024 * 1024
        ),
        name="phase_exchange",
    )(parts)


def grad_exchange_kernel(tiles, slabs, grad_ref, out_ref, came, slab_send, slab_recv, tile_send, tile_recv):
    pairs = grad_ref.shape[0]
    slices = out_ref.shape[3]
    me_t = lax.axis_index("tile")
    me_s = lax.axis_index("slab")
    greet((("tile", tiles), ("slab", slabs)))

    def rows_of(slab):
        return pl.ds(pl.multiple_of(slab * slices, slices), slices)

    def slab_copy(p, step):
        peer = lax.rem(me_s + step, slabs)
        return pltpu.make_async_remote_copy(
            src_ref=grad_ref.at[p, :, rows_of(peer), :],
            dst_ref=came.at[step - 1, p],
            send_sem=slab_send.at[step - 1, p],
            recv_sem=slab_recv.at[step - 1, p],
            device_id={"slab": peer},
            device_id_type=MESH,
        )

    def tile_copy(p, step):
        return pltpu.make_async_remote_copy(
            src_ref=out_ref.at[me_t, p],
            dst_ref=out_ref.at[me_t, p],
            send_sem=tile_send.at[step - 1, p],
            recv_sem=tile_recv.at[step - 1, p],
            device_id={"tile": lax.rem(me_t + step, tiles)},
            device_id_type=MESH,
        )

    for p in range(pairs):
        for step in range(1, slabs):
            slab_copy(p, step).start()
    for p in range(pairs):
        total = grad_ref[p, :, rows_of(me_s), :].astype(F32)
        for step in range(1, slabs):
            slab_copy(p, step).wait_recv()
            total += came[step - 1, p].astype(F32)
        out_ref[me_t, p] = total.astype(WIRE)
        for step in range(1, tiles):
            tile_copy(p, step).start()
    for p in range(pairs):
        for step in range(1, tiles):
            tile_copy(p, step).wait_recv()
    for p in range(pairs):
        for step in range(1, tiles):
            tile_copy(p, step).wait_send()
        for step in range(1, slabs):
            slab_copy(p, step).wait_send()


def grad_exchange(grads, tiles, slabs):
    pairs, pieces, all_rows = grads.shape[:3]
    slices = all_rows // slabs
    return pl.pallas_call(
        functools.partial(grad_exchange_kernel, tiles, slabs),
        out_shape=jax.ShapeDtypeStruct((tiles, pairs, pieces, slices, LANES), WIRE),
        in_specs=[pl.BlockSpec(memory_space=pltpu.VMEM)],
        out_specs=pl.BlockSpec(memory_space=pltpu.VMEM),
        scratch_shapes=[
            pltpu.VMEM((slabs - 1, pairs, pieces, slices, LANES), WIRE),
            pltpu.SemaphoreType.DMA((slabs - 1, pairs)),
            pltpu.SemaphoreType.DMA((slabs - 1, pairs)),
            pltpu.SemaphoreType.DMA((tiles - 1, pairs)),
            pltpu.SemaphoreType.DMA((tiles - 1, pairs)),
        ],
        compiler_params=pltpu.CompilerParams(
            collective_id=1, has_side_effects=True, vmem_limit_bytes=16 * 1024 * 1024
        ),
        name="grad_exchange",
    )(grads)


def sin_cos(phase):
    turns = phase * (0.5 / math.pi)
    turns = turns - jnp.round(turns)
    square = turns * turns
    sine, cosine = SIN_POLY[-1], COS_POLY[-1]
    for low_s, low_c in zip(SIN_POLY[-2::-1], COS_POLY[-2::-1]):
        sine = sine * square + low_s
        cosine = cosine * square + low_c
    sine = sine * turns
    double = sine + sine
    return double * cosine, 1.0 - double * sine


def frame_kernel(
    own, owner_ref, start_ref, phase_ref, probe_ref, measured_ref,
    right_ref, left_ref, left_back_ref, right_back_ref, out_ref, acc,
):
    pairs = phase_ref.shape[0]
    frames, side, unused = measured_ref.shape
    ring = own + 1
    acc[...] = jnp.zeros_like(acc)
    lanes = lane_ids((side, LANES))

    def place(member):
        angle = owner_ref[member, 0]
        start = start_ref[member]
        start = jnp.where(start < 0, start + ring * LANES, start)
        first = start // LANES
        offset = start - first * LANES
        second = jnp.where(first + 1 == ring, 0, first + 1)
        return angle, first, second, offset

    def piece(angle, block, offset):
        upper = jnp.where(angle >= pairs, 1, 0)
        pair = angle - upper * pairs
        margin = block == own
        index = jnp.where(margin, 2 * own, upper * own + block)
        turn = jnp.where(margin, upper * HALF, 0) + LANES - offset
        turn = jnp.where(turn >= LANES, turn - LANES, turn)
        return pltpu.roll(phase_ref[pair, index].astype(F32), turn, 1)

    def step(number, carried):
        for duo in range(GROUP // 2):
            two = [number * GROUP + 2 * duo, number * GROUP + 2 * duo + 1]
            waves = []
            for member in two:
                angle, first, second, offset = place(member)
                window = jnp.where(
                    lanes < LANES - offset, piece(angle, first, offset), piece(angle, second, offset)
                )
                sine, cosine = sin_cos(window)
                probe_re, probe_im = probe_ref[0], probe_ref[1]
                waves.append((probe_re * cosine - probe_im * sine, probe_re * sine + probe_im * cosine))
            stacked = jnp.concatenate(
                [jnp.concatenate([re.astype(BF16), im.astype(BF16)], axis=1) for re, im in waves], axis=0
            )
            half = jnp.dot(stacked, right_ref[...], preferred_element_type=F32).astype(BF16)

            def by_lane(value):
                return jnp.concatenate(
                    [
                        jnp.concatenate([value[:side, :LANES], value[side:, :LANES]], axis=1),
                        jnp.concatenate([value[:side, LANES:], value[side:, LANES:]], axis=1),
                    ],
                    axis=0,
                )

            far = jnp.dot(left_ref[...], by_lane(half), preferred_element_type=F32)
            far_re, far_im = far[:side], far[side:]
            amplitude = jnp.concatenate([measured_ref[member] for member in two], axis=1).astype(F32)
            factor = 1.0 - amplitude * lax.rsqrt(far_re * far_re + far_im * far_im + SMOOTHING)
            resid = jnp.concatenate([(far_re * factor).astype(BF16), (far_im * factor).astype(BF16)], axis=0)
            back = jnp.dot(left_back_ref[...], resid, preferred_element_type=F32).astype(BF16)
            near = jnp.dot(by_lane(back), right_back_ref[...], preferred_element_type=F32)
            for slot, member in enumerate(two):
                wave_re, wave_im = waves[slot]
                cut = slice(slot * side, (slot + 1) * side)
                grad = near[cut, LANES:] * wave_re - near[cut, :LANES] * wave_im
                angle, first, second, offset = place(member)
                turned = pltpu.roll(grad, offset, 1)
                kept = lanes >= offset
                acc[angle, first] += jnp.where(kept, turned, 0.0)
                acc[angle, second] += jnp.where(kept, 0.0, turned)
        return carried

    lax.fori_loop(0, frames // GROUP, step, 0)
    for p in range(pairs):
        for hi in range(2):
            for b in range(own):
                out_ref[p, hi * own + b] = acc[p + hi * pairs, b].astype(WIRE)
        out_ref[p, 2 * own] = halo_join(acc[p, own], acc[p + pairs, own]).astype(WIRE)


def complex_tables(length):
    indices = jnp.arange(length, dtype=jnp.int32)
    product = indices[:, None] * indices[None, :] % length
    phases = product.astype(F32) * (2.0 * math.pi / length)
    cosine, sine = jnp.cos(phases), jnp.sin(phases)
    plus = jnp.block([[cosine, sine], [-sine, cosine]])
    minus = jnp.block([[cosine, -sine], [sine, cosine]])
    scale = 1.0 / length
    return minus.astype(BF16), (plus * scale).astype(BF16), minus.astype(BF16), (plus * scale).astype(BF16)


def frame_gradients(owner, shift, phases, probe, measured, own):
    pairs, pieces, rows, unused = phases.shape
    tables = complex_tables(LANES)
    smem = pl.BlockSpec(memory_space=pltpu.SMEM)
    vmem = pl.BlockSpec(memory_space=pltpu.VMEM)
    return pl.pallas_call(
        functools.partial(frame_kernel, own),
        out_shape=jax.ShapeDtypeStruct(phases.shape, WIRE),
        in_specs=[smem, smem] + [vmem] * 7,
        out_specs=vmem,
        scratch_shapes=[pltpu.VMEM((2 * pairs, own + 1, rows, LANES), F32)],
        compiler_params=pltpu.CompilerParams(vmem_limit_bytes=48 * 1024 * 1024),
        name="frames",
    )(owner, shift, phases, probe, measured, *tables)


def backproject_kernel(slices, blocks, beams, shears_ref, shift_ref, grad_ref, out_ref, near, far, rows_f32, lhs, ker):
    tiles, pairs, pieces = grad_ref.shape[:3]
    angles = 2 * pairs
    own = (pieces - 1) // 2
    half_rows = slices * blocks
    group = pl.program_id(0)
    lanes = lane_ids((slices, LANES))

    @pl.when(group == 0)
    def prepare():
        zero = jnp.zeros((slices, LANES), F32)
        for edge in (0, blocks + 1, blocks + 2):
            near[edge] = zero
            far[edge] = zero
        for a in range(angles):
            hi, p = a // pairs, a % pairs
            margins = []
            for t in range(tiles):
                margin = grad_ref[t, p, 2 * own].astype(F32)
                margins.append(pltpu.roll(margin, HALF, 1) if hi else margin)
            for t in range(tiles):
                for b in range(own):
                    value = grad_ref[t, p, hi * own + b].astype(F32)
                    if b == 0 and t > 0:
                        value += jnp.where(lanes < HALO, margins[t - 1], 0.0)
                    if b == own - 1 and t + 1 < tiles:
                        value += jnp.where(lanes >= LANES - HALO, margins[t + 1], 0.0)
                    k = t * own + b + 1
                    near[k] = pltpu.roll(value, LANES - HALO, 1)
                    far[k] = pltpu.roll(value, LANES - HALO - HALF, 1)
            shift = shift_ref[a, 0]
            for i in range(blocks):
                k = i + 1 + shift
                lower = jnp.where(lanes < LANES - HALO, near[k], near[k + 1])
                upper = jnp.where(lanes < LANES - HALO - HALF, far[k], far[k + 1])
                rows_f32[pl.ds(i, slices, stride=blocks), :] = lower
                rows_f32[pl.ds(half_rows + i, slices, stride=blocks), :] = upper
            lhs[:, a * LANES : (a + 1) * LANES] = rows_f32[...].astype(BF16)

    shape = (LANES, LANES)
    base = (row_ids(shape) - lane_ids(shape) % HALF - HALO).astype(F32) * ROOT
    pick = (lane_ids((1, LANES)) >= HALF).astype(F32)
    for a in range(angles):
        slope = shears_ref[a] * ROOT
        for pair in range(4):
            place = (group * 8 + 2 * pair).astype(F32) - (beams - 1) * 0.5
            gap = base - (pick + place) * slope
            ker[a * LANES : (a + 1) * LANES, pair * LANES : (pair + 1) * LANES] = jnp.exp2(-(gap * gap)).astype(BF16)
    result = jnp.dot(lhs[...], ker[...], preferred_element_type=F32)
    left = lane_ids((half_rows, LANES)) < HALF
    for pair in range(4):
        cols = slice(pair * LANES, (pair + 1) * LANES)
        lower, upper = result[:half_rows, cols], result[half_rows:, cols]
        crossed = pltpu.roll(jnp.where(left, upper, lower), HALF, 1)
        first = jnp.where(left, lower, crossed)
        second = jnp.where(left, crossed, upper)
        for s in range(slices):
            cut = slice(s * blocks, (s + 1) * blocks)
            out_ref[s, 0, pl.ds(2 * pair, blocks, stride=8), :] = first[cut]
            out_ref[s, 0, pl.ds(2 * pair + 1, blocks, stride=8), :] = second[cut]


def backproject(shears, tile_shift, grads, slices, beams, blocks):
    tiles, pairs = grads.shape[:2]
    angles = 2 * pairs
    rows = 2 * slices * blocks
    smem = pl.BlockSpec(memory_space=pltpu.SMEM)
    groups = beams // 8
    result = pl.pallas_call(
        functools.partial(backproject_kernel, slices, blocks, beams),
        out_shape=jax.ShapeDtypeStruct((slices, groups, blocks * 8, LANES), F32),
        grid=(groups,),
        in_specs=[smem, smem, pl.BlockSpec(memory_space=pltpu.VMEM)],
        out_specs=pl.BlockSpec((slices, 1, blocks * 8, LANES), lambda g: (0, g, 0, 0)),
        scratch_shapes=[
            pltpu.VMEM((blocks + 3, slices, LANES), F32),
            pltpu.VMEM((blocks + 3, slices, LANES), F32),
            pltpu.VMEM((rows, LANES), F32),
            pltpu.VMEM((rows, angles * LANES), BF16),
            pltpu.VMEM((angles * LANES, 4 * LANES), BF16),
        ],
        compiler_params=pltpu.CompilerParams(vmem_limit_bytes=48 * 1024 * 1024),
        name="backproject",
    )(shears, tile_shift, grads)
    result = result.reshape(slices, groups, blocks, 8, LANES).transpose(0, 1, 3, 2, 4)
    return result.reshape(slices, beams, blocks * LANES)


def body(volume, shears, tile_shift, illumination, measured, frame_owner, frame_shift):
    tiles, slabs = lax.axis_size("tile"), lax.axis_size("slab")
    slices, beams, width = volume.shape
    blocks = width // LANES
    parts = project(shears, tile_shift, volume, tiles)
    phases = phase_exchange(parts, tiles, slabs)
    grads = frame_gradients(frame_owner, frame_shift, phases, illumination, measured, blocks // tiles)
    gathered = grad_exchange(grads, tiles, slabs)
    return backproject(shears, tile_shift, gathered, slices, beams, blocks)


def solution(mesh):
    in_specs = (
        P("slab", "tile", None),
        P(),
        P(None, "tile"),
        P(),
        P(("slab", "tile"), None, None),
        P(("slab", "tile"), None),
        P(("slab", "tile")),
    )
    out_specs = P("slab", "tile", None)
    return jax.shard_map(body, mesh=mesh, in_specs=in_specs, out_specs=out_specs, check_vma=False)
```

profile of v0, /device:TPU:0, one launch (start us, length us, event | category | flops | bytes accessed | tf_op | source)
XLA Modules:
  0.0 72.5 jit_solution(10259118730182613349)
XLA Ops:
  0.0 0.0 copy-start.5
  0.0 0.0 copy-start.2
  0.0 0.8 %copy.10.shift_ref = s32[8,1]{1,0:T(8,128)S(1)} copy(s32[8,1]{0,1:T(1,128)} %param.9) | data formatting | bytes 64 | tf_op args[2]
  0.8 0.7 %copy.9.owner_ref = s32[32,1]{1,0:T(8,128)S(1)} copy(s32[32,1]{0,1:T(1,128)} %param.12) | data formatting | bytes 256 | tf_op args[5]
  1.5 0.3 fusion.12
  1.8 0.3 fusion.10
  2.0 0.3 fusion.9
  2.3 0.3 fusion.7
  2.6 0.0 copy-start
  2.6 2.2 %copy-done = f32[16,64,1024]{2,1,0:T(8,128)S(1)} copy-done((f32[16,64,1024]{2,1,0:T(8,128)S(1)}, f32[16,64,1024]{2,1,0:T(8,128)}, u32[]{:S(2)}) %copy-start) | copy-done | bytes 4194328
  4.8 0.0 copy-start.3
  4.8 0.7 copy-done.3
  5.5 0.0 copy-start.1
  5.5 0.0 copy-start.4
  5.5 11.8 %project.1.part_ref = bf16[4,4,5,16,128]{4,3,2,1,0:T(8,128)(2,1)S(1)} custom-call(f32[8]{0:T(128)S(1)} %copy-done.3, s32[8,1]{1,0:T(8,128)S(1)} %copy.10.shift_ref, f32[8192,128]{1,0:T(8,128)S(1)} %bitcast.10), custom_call_target="tpu_custom_call" | custom-call | tf_op jit(solution)/shard_map/project/pallas_call | solution.py:121
  17.3 18.8 %phase_exchange.1.phase_ref = bf16[4,5,128,128]{3,2,1,0:T(8,128)(2,1)S(1)} custom-call(bf16[4,4,5,16,128]{4,3,2,1,0:T(8,128)(2,1)S(1)} %project.1.part_ref), custom_call_target="tpu_custom_call" | custom-call | tf_op jit(solution)/shard_map/phase_exchange/pallas_call | solution.py:206
  36.1 0.0 copy-done.5
  36.1 0.0 copy-done.2
  36.1 0.0 copy-done.1
  36.1 11.1 %frames.1.grad_ref = bf16[4,5,128,128]{3,2,1,0:T(8,128)(2,1)S(1)} custom-call(s32[32,1]{1,0:T(8,128)S(1)} %copy.9.owner_ref, s32[32]{0:T(128)S(1)} %copy-done.5, bf16[4,5,128,128]{3,2,1,0:T(8,128)(2,1)S(1)} %phase_exchange.1.phase_ref, f32[2,128,128]{2,1,0:T(8,128)S(1)} %copy-done.2, bf16[32,128,128]{2,1,0:T(8,128)(2,1)S(1)} %copy-done.1, ...), custom_call_target="tpu_custom_call" | custom-call | tf_op jit(solution)/shard_map/frames/pallas_call | solution.py:408
  47.2 16.1 %grad_exchange.1.grad_ref = bf16[4,4,5,16,128]{4,3,2,1,0:T(8,128)(2,1)S(1)} custom-call(bf16[4,5,128,128]{3,2,1,0:T(8,128)(2,1)S(1)} %frames.1.grad_ref), custom_call_target="tpu_custom_call" | custom-call | tf_op jit(solution)/shard_map/grad_exchange/pallas_call | solution.py:280
  63.2 0.0 copy-done.4
  63.3 9.2 %backproject.1 = f32[16,8,64,128]{3,2,1,0:T(8,128)} custom-call(f32[8]{0:T(128)S(1)} %copy-done.4, s32[8,1]{1,0:T(8,128)S(1)} %copy.10.shift_ref, bf16[4,4,5,16,128]{4,3,2,1,0:T(8,128)(2,1)S(1)} %grad_exchange.1.grad_ref), custom_call_target="tpu_custom_call" | custom-call | tf_op jit(solution)/shard_map/backproject/pallas_call | solution.py:487
  (2 shorter events, 0.0 us)
Async XLA Ops:
  0.0 36.1 %copy-start.5 = (s32[32]{0:T(128)S(1)}, s32[32]{0:T(128)}, u32[]{:S(2)}) copy-start(s32[32]{0:T(128)} %start_ref.1) | copy-start | bytes 388
  0.0 36.1 %copy-start.2 = (f32[2,128,128]{2,1,0:T(8,128)S(1)}, f32[2,128,128]{2,1,0:T(8,128)}, u32[]{:S(2)}) copy-start(f32[2,128,128]{2,1,0:T(8,128)} %probe_ref.1) | copy-start | bytes 393220
  2.6 2.2 %copy-start = (f32[16,64,1024]{2,1,0:T(8,128)S(1)}, f32[16,64,1024]{2,1,0:T(8,128)}, u32[]{:S(2)}) copy-start(f32[16,64,1024]{2,1,0:T(8,128)} %param.7) | copy-start | bytes 12582916
  4.8 0.7 copy-start.3
  5.5 30.6 %copy-start.1 = (bf16[32,128,128]{2,1,0:T(8,128)(2,1)S(1)}, bf16[32,128,128]{2,1,0:T(8,128)(2,1)}, u32[]{:S(2)}) copy-start(bf16[32,128,128]{2,1,0:T(8,128)(2,1)} %measured_ref.1) | copy-start | bytes 3145732
  5.5 57.8 %copy-start.4 = (f32[8]{0:T(128)S(1)}, f32[8]{0:T(128)}, u32[]{:S(2)}) copy-start(f32[8]{0:T(128)} %shears_ref.3) | copy-start | bytes 100
where the time goes:
time: 72.7 us; the launch traced here: 72.5 us
  Pallas kernels  66.9 us (92%)
  local copies, waits for them, and re-layouts  4.35 us (6%)
  other arithmetic  1.1 us (2%)
    pallas_call x1, Pallas kernels, phase_exchange(): pl.pallas_call(functools.partial(phase_exchange_kernel, tiles, slabs), ou...  18.8 us
    pallas_call x1, Pallas kernels, grad_exchange(): pl.pallas_call(functools.partial(grad_exchange_kernel, tiles, slabs), out...  16.1 us
    pallas_call x1, Pallas kernels, project(): pl.pallas_call(functools.partial(project_kernel, tiles, slices, beams, bl...  11.8 us
    pallas_call x1, Pallas kernels, frame_gradients(): pl.pallas_call(functools.partial(frame_kernel, own), out_shape=jax.ShapeD...  11.1 us
    pallas_call x1, Pallas kernels, backproject(): pl.pallas_call(functools.partial(backproject_kernel, slices, blocks, beam...  9.22 us
    unnamed x14, local copies, waits for them, and re-layouts  4.35 us

commit v1 on v0

v1 whole, which is shorter than its diff:
```python
import functools
import math

import jax
import jax.numpy as jnp
import numpy as np
from jax import lax
from jax.experimental import pallas as pl
from jax.experimental.pallas import tpu as pltpu
from jax.sharding import PartitionSpec as P

LANES = 128
HALF = LANES // 2
HALO = 32
SMOOTHING = 0.25
WIRE = jnp.bfloat16
F32 = jnp.float32
BF16 = jnp.bfloat16
MESH = pl.DeviceIdType.MESH
ROOT = math.sqrt(0.5 * math.log2(math.e))
GROUP = 8
SIN_POLY = (3.1415926401307073, -5.1677100835078775, 2.550077523214199, -0.5982912856179897, 0.07765766030124945)
COS_POLY = (0.9999999532476078, -4.934792830619626, 4.0584113528622625, -1.331876568078962, 0.2196896110945085)


def lane_ids(shape):
    return lax.broadcasted_iota(jnp.int32, shape, len(shape) - 1)


def row_ids(shape):
    return lax.broadcasted_iota(jnp.int32, shape, len(shape) - 2)


def halo_join(low, high):
    lanes = lane_ids(low.shape)
    outer = (lanes < HALO) | (lanes >= LANES - HALO)
    return jnp.where(outer, low, pltpu.roll(high, HALF, 1))


def signal_peers(axes):
    barrier = pltpu.get_barrier_semaphore()
    total = 0
    for axis, count in axes:
        me = lax.axis_index(axis)
        for step in range(1, count):
            pl.semaphore_signal(
                barrier, inc=1, device_id={axis: lax.rem(me + step, count)}, device_id_type=MESH
            )
            total += 1
    return barrier, total


def sin_cos(phase):
    turns = phase * (0.5 / math.pi)
    turns = turns - jnp.round(turns)
    square = turns * turns
    sine, cosine = SIN_POLY[-1], COS_POLY[-1]
    for low_s, low_c in zip(SIN_POLY[-2::-1], COS_POLY[-2::-1]):
        sine = sine * square + low_s
        cosine = cosine * square + low_c
    sine = sine * turns
    double = sine + sine
    return double * cosine, 1.0 - double * sine


def phase_kernel(
    tiles, slabs, slices, beams, blocks,
    shears_hbm, shift_hbm, v_hbm, cos_ref, sin_ref,
    shears_ref, shift_ref, v_ref, lhs, ker, res, comb, parts, came, phase,
    small_sem, volume_sem, tile_send, tile_recv, slab_send, slab_recv,
):
    pairs = phase.shape[0]
    own = blocks // tiles
    groups = beams // 8
    half_rows = slices * blocks
    me_t = lax.axis_index("tile")
    me_s = lax.axis_index("slab")
    rows = pl.ds(pl.multiple_of(me_s * slices, slices), slices)

    small = [
        pltpu.make_async_copy(shears_hbm, shears_ref, small_sem.at[0]),
        pltpu.make_async_copy(shift_hbm, shift_ref, small_sem.at[1]),
    ]
    for copy in small:
        copy.start()

    def volume_copy(group):
        return pltpu.make_async_copy(v_hbm.at[:, group], v_ref.at[group], volume_sem.at[group])

    for group in range(groups):
        volume_copy(group).start()
    barrier, greetings = signal_peers((("tile", tiles), ("slab", slabs)))

    def tile_copy(p, step):
        peer = lax.rem(me_t + step, tiles)
        return pltpu.make_async_remote_copy(
            src_ref=parts.at[peer, p],
            dst_ref=came.at[step - 1, p],
            send_sem=tile_send.at[step - 1, p],
            recv_sem=tile_recv.at[step - 1, p],
            device_id={"tile": peer},
            device_id_type=MESH,
        )

    def slab_copy(p, step):
        return pltpu.make_async_remote_copy(
            src_ref=phase.at[p, :, rows, :],
            dst_ref=phase.at[p, :, rows, :],
            send_sem=slab_send.at[step - 1, p],
            recv_sem=slab_recv.at[step - 1, p],
            device_id={"slab": lax.rem(me_s + step, slabs)},
            device_id_type=MESH,
        )

    def arrange(group, carried):
        volume_copy(group).wait()
        for pair in range(4):
            col = pl.multiple_of((group * 4 + pair) * LANES, LANES)
            for duo in range(slices // 2):
                lower, upper = [], []
                for s in (2 * duo, 2 * duo + 1):
                    first = v_ref[group, s, pl.ds(2 * pair, blocks, stride=8), :]
                    second = v_ref[group, s, pl.ds(2 * pair + 1, blocks, stride=8), :]
                    left = lane_ids(first.shape) < HALF
                    crossed = pltpu.roll(jnp.where(left, second, first), HALF, 1)
                    lower.append(jnp.where(left, first, crossed))
                    upper.append(jnp.where(left, crossed, second))
                row = 2 * duo * blocks
                lhs[row : row + 2 * blocks, pl.ds(col, LANES)] = jnp.concatenate(lower, 0).astype(BF16)
                row += half_rows
                lhs[row : row + 2 * blocks, pl.ds(col, LANES)] = jnp.concatenate(upper, 0).astype(BF16)
        return carried

    shape = (HALF, LANES)
    base = (lane_ids(shape) - row_ids(shape) - HALO).astype(F32) * ROOT
    lanes = lane_ids((half_rows, LANES))
    lanes_s = lane_ids((slices, LANES))
    zero = jnp.zeros((slices, LANES), F32)

    def make_beams(p):
        steps = [shears_ref[p] * ROOT, shears_ref[p + pairs] * ROOT]

        def beam(q, carried):
            place = q.astype(F32) - (beams - 1) * 0.5
            row = pl.multiple_of(q * HALF, HALF)
            for side in range(2):
                gap = base - place * steps[side]
                ker[pl.ds(row, HALF), side * LANES : (side + 1) * LANES] = jnp.exp2(-(gap * gap)).astype(BF16)
            return carried

        lax.fori_loop(0, beams, beam, 0, unroll=8)

    def shifted_sums(p, side):
        cols = slice(side * LANES, (side + 1) * LANES)
        near = pltpu.roll(res[0:half_rows, cols], HALO, 1)
        far = pltpu.roll(res[half_rows : 2 * half_rows, cols], HALO + HALF, 1)
        comb[side, 0] = jnp.where(lanes >= HALO, near, 0.0) + jnp.where(lanes >= HALO + HALF, far, 0.0)
        comb[side, 1] = jnp.where(lanes < HALO, near, 0.0) + jnp.where(lanes < HALO + HALF, far, 0.0)
        shift = shift_ref[p + side * pairs]
        row_of = []
        for k in range(blocks):
            total = zero
            for o in range(2):
                i = k - shift - o
                inside = (i >= 0) & (i < blocks)
                picked = comb[side, o, pl.ds(jnp.clip(i, 0, blocks - 1), slices, stride=blocks), :]
                total += jnp.where(inside, picked, 0.0)
            row_of.append(total)
        return row_of

    def project_pair(p):
        res[...] = jnp.dot(lhs[...], ker[...], preferred_element_type=F32)
        sums = [shifted_sums(p, side) for side in range(2)]
        for t in range(tiles):
            margins = []
            for side in range(2):
                for b in range(own):
                    parts[t, p, side * own + b] = sums[side][t * own + b].astype(WIRE)
                after = sums[side][(t + 1) * own] if t + 1 < tiles else zero
                before = sums[side][t * own - 1] if t > 0 else zero
                margins.append(jnp.where(lanes_s < HALF, after, before))
            parts[t, p, 2 * own] = halo_join(margins[0], margins[1]).astype(WIRE)

    for copy in small:
        copy.wait()
    make_beams(0)
    lax.fori_loop(0, groups, arrange, 0)
    project_pair(0)
    pl.semaphore_wait(barrier, greetings)
    for p in range(pairs):
        if p:
            make_beams(p)
            project_pair(p)
        for step in range(1, tiles):
            tile_copy(p, step).start()
    for p in range(pairs):
        total = parts[me_t, p].astype(F32)
        for step in range(1, tiles):
            tile_copy(p, step).wait_recv()
            total += came[step - 1, p].astype(F32)
        phase[p, :, rows, :] = total.astype(WIRE)
        for step in range(1, slabs):
            slab_copy(p, step).start()
    for p in range(pairs):
        for step in range(1, slabs):
            slab_copy(p, step).wait_recv()

        def wave_piece(piece, carried):
            sine, cosine = sin_cos(phase[p, piece].astype(F32))
            sin_ref[p, piece] = sine
            cos_ref[p, piece] = cosine
            return carried

        lax.fori_loop(0, phase.shape[1], wave_piece, 0)
    for p in range(pairs):
        for step in range(1, tiles):
            tile_copy(p, step).wait_send()
        for step in range(1, slabs):
            slab_copy(p, step).wait_send()


def phase_waves(shears, tile_shift, volume, tiles, slabs):
    slices, beams, width = volume.shape
    blocks = width // LANES
    angles = shears.shape[0]
    pairs, own, groups = angles // 2, blocks // tiles, beams // 8
    pieces = 2 * own + 1
    view = volume.reshape(slices, groups, 8, blocks, LANES).transpose(0, 1, 3, 2, 4)
    view = view.reshape(slices, groups, blocks * 8, LANES)
    rows = 2 * slices * blocks
    waves = jax.ShapeDtypeStruct((pairs, pieces, slabs * slices, LANES), F32)
    return pl.pallas_call(
        functools.partial(phase_kernel, tiles, slabs, slices, beams, blocks),
        out_shape=(waves, waves),
        in_specs=[pl.BlockSpec(memory_space=pltpu.HBM)] * 3,
        out_specs=(pl.BlockSpec(memory_space=pltpu.VMEM),) * 2,
        scratch_shapes=[
            pltpu.SMEM((angles,), F32),
            pltpu.SMEM((angles,), jnp.int32),
            pltpu.VMEM((groups, slices, blocks * 8, LANES), F32),
            pltpu.VMEM((rows, beams * HALF), BF16),
            pltpu.VMEM((beams * HALF, 2 * LANES), BF16),
            pltpu.VMEM((rows, 2 * LANES), F32),
            pltpu.VMEM((2, 2, rows // 2, LANES), F32),
            pltpu.VMEM((tiles, pairs, pieces, slices, LANES), WIRE),
            pltpu.VMEM((tiles - 1, pairs, pieces, slices, LANES), WIRE),
            pltpu.VMEM((pairs, pieces, slabs * slices, LANES), WIRE),
            pltpu.SemaphoreType.DMA((2,)),
            pltpu.SemaphoreType.DMA((groups,)),
            pltpu.SemaphoreType.DMA((tiles - 1, pairs)),
            pltpu.SemaphoreType.DMA((tiles - 1, pairs)),
            pltpu.SemaphoreType.DMA((slabs - 1, pairs)),
            pltpu.SemaphoreType.DMA((slabs - 1, pairs)),
        ],
        compiler_params=pltpu.CompilerParams(
            collective_id=0, has_side_effects=True, vmem_limit_bytes=40 * 1024 * 1024
        ),
        name="phase_waves",
    )(
        pltpu.with_memory_space_constraint(shears, pltpu.HBM),
        pltpu.with_memory_space_constraint(tile_shift, pltpu.HBM),
        pltpu.with_memory_space_constraint(view, pltpu.HBM),
    )


def grad_kernel(
    tiles, slabs, blocks, beams,
    shears_ref, shift_ref, grad_ref, lhs_ref, ker_ref,
    gathered, near, far, rows_f32, came, slab_send, slab_recv, tile_send, tile_recv,
):
    pairs, pieces = grad_ref.shape[:2]
    own = (pieces - 1) // 2
    slices = gathered.shape[3]
    half_rows = slices * blocks
    me_t = lax.axis_index("tile")
    me_s = lax.axis_index("slab")
    barrier, greetings = signal_peers((("tile", tiles), ("slab", slabs)))
    pl.semaphore_wait(barrier, greetings)

    def rows_of(slab):
        return pl.ds(pl.multiple_of(slab * slices, slices), slices)

    def slab_copy(p, step):
        peer = lax.rem(me_s + step, slabs)
        return pltpu.make_async_remote_copy(
            src_ref=grad_ref.at[p, :, rows_of(peer), :],
            dst_ref=came.at[step - 1, p],
            send_sem=slab_send.at[step - 1, p],
            recv_sem=slab_recv.at[step - 1, p],
            device_id={"slab": peer},
            device_id_type=MESH,
        )

    def tile_copy(p, step):
        return pltpu.make_async_remote_copy(
            src_ref=gathered.at[me_t, p],
            dst_ref=gathered.at[me_t, p],
            send_sem=tile_send.at[step - 1, p],
            recv_sem=tile_recv.at[step - 1, p],
            device_id={"tile": lax.rem(me_t + step, tiles)},
            device_id_type=MESH,
        )

    for p in range(pairs):
        for step in range(1, slabs):
            slab_copy(p, step).start()

    shape = (LANES, LANES)
    base = (row_ids(shape) - lane_ids(shape) % HALF - HALO).astype(F32) * ROOT
    pick = (lane_ids((1, LANES)) >= HALF).astype(F32) - (beams - 1) * 0.5
    for a in range(2 * pairs):
        slope = shears_ref[a] * ROOT

        def beam(pair, carried):
            gap = base - (pick + (2 * pair).astype(F32)) * slope
            col = pl.multiple_of(pair * LANES, LANES)
            ker_ref[a * LANES : (a + 1) * LANES, pl.ds(col, LANES)] = jnp.exp2(-(gap * gap)).astype(BF16)
            return carried

        lax.fori_loop(0, beams // 2, beam, 0, unroll=8)

    for p in range(pairs):
        total = grad_ref[p, :, rows_of(me_s), :].astype(F32)
        for step in range(1, slabs):
            slab_copy(p, step).wait_recv()
            total += came[step - 1, p].astype(F32)
        gathered[me_t, p] = total.astype(WIRE)
        for step in range(1, tiles):
            tile_copy(p, step).start()

    lanes = lane_ids((slices, LANES))
    zero = jnp.zeros((slices, LANES), F32)
    for edge in (0, blocks + 1, blocks + 2):
        near[edge] = zero
        far[edge] = zero
    for p in range(pairs):
        for step in range(1, tiles):
            tile_copy(p, step).wait_recv()
        for hi in range(2):
            a = p + hi * pairs
            margins = []
            for t in range(tiles):
                margin = gathered[t, p, 2 * own].astype(F32)
                margins.append(pltpu.roll(margin, HALF, 1) if hi else margin)
            for t in range(tiles):
                for b in range(own):
                    value = gathered[t, p, hi * own + b].astype(F32)
                    if b == 0 and t > 0:
                        value += jnp.where(lanes < HALO, margins[t - 1], 0.0)
                    if b == own - 1 and t + 1 < tiles:
                        value += jnp.where(lanes >= LANES - HALO, margins[t + 1], 0.0)
                    k = t * own + b + 1
                    near[k] = pltpu.roll(value, LANES - HALO, 1)
                    far[k] = pltpu.roll(value, LANES - HALO - HALF, 1)
            shift = shift_ref[a]
            for i in range(blocks):
                k = i + 1 + shift
                lower = jnp.where(lanes < LANES - HALO, near[k], near[k + 1])
                upper = jnp.where(lanes < LANES - HALO - HALF, far[k], far[k + 1])
                rows_f32[pl.ds(i, slices, stride=blocks), :] = lower
                rows_f32[pl.ds(half_rows + i, slices, stride=blocks), :] = upper
            lhs_ref[:, a * LANES : (a + 1) * LANES] = rows_f32[...].astype(BF16)
    for p in range(pairs):
        for step in range(1, tiles):
            tile_copy(p, step).wait_send()
        for step in range(1, slabs):
            slab_copy(p, step).wait_send()


def back_operands(shears, tile_shift, grads, tiles, slabs, blocks, beams):
    pairs, pieces, all_rows = grads.shape[:3]
    slices = all_rows // slabs
    angles = 2 * pairs
    rows = 2 * slices * blocks
    smem = pl.BlockSpec(memory_space=pltpu.SMEM)
    vmem = pl.BlockSpec(memory_space=pltpu.VMEM)
    return pl.pallas_call(
        functools.partial(grad_kernel, tiles, slabs, blocks, beams),
        out_shape=(
            jax.ShapeDtypeStruct((rows, angles * LANES), BF16),
            jax.ShapeDtypeStruct((angles * LANES, beams * HALF), BF16),
        ),
        in_specs=[smem, smem, vmem],
        out_specs=(vmem, vmem),
        scratch_shapes=[
            pltpu.VMEM((tiles, pairs, pieces, slices, LANES), WIRE),
            pltpu.VMEM((blocks + 3, slices, LANES), F32),
            pltpu.VMEM((blocks + 3, slices, LANES), F32),
            pltpu.VMEM((rows, LANES), F32),
            pltpu.VMEM((slabs - 1, pairs, pieces, slices, LANES), WIRE),
            pltpu.SemaphoreType.DMA((slabs - 1, pairs)),
            pltpu.SemaphoreType.DMA((slabs - 1, pairs)),
            pltpu.SemaphoreType.DMA((tiles - 1, pairs)),
            pltpu.SemaphoreType.DMA((tiles - 1, pairs)),
        ],
        compiler_params=pltpu.CompilerParams(
            collective_id=1, has_side_effects=True, vmem_limit_bytes=40 * 1024 * 1024
        ),
        name="back_operands",
    )(shears, tile_shift, grads)


def frame_kernel(
    own, owner_ref, start_ref, cos_ref, sin_ref, probe_ref, measured_ref, minus_ref, plus_ref, out_ref, acc,
):
    pairs = cos_ref.shape[0]
    frames, side, unused = measured_ref.shape
    ring = own + 1
    acc[...] = jnp.zeros_like(acc)
    lanes = lane_ids((side, LANES))

    def place(member):
        angle = owner_ref[member]
        start = start_ref[member]
        start = jnp.where(start < 0, start + ring * LANES, start)
        first = start // LANES
        offset = start - first * LANES
        second = jnp.where(first + 1 == ring, 0, first + 1)
        return angle, first, second, offset

    def source(angle, block, offset):
        upper = jnp.where(angle >= pairs, 1, 0)
        margin = block == own
        index = jnp.where(margin, 2 * own, upper * own + block)
        turn = jnp.where(margin, upper * HALF, 0) + LANES - offset
        return angle - upper * pairs, index, jnp.where(turn >= LANES, turn - LANES, turn)

    def by_lane(value):
        return jnp.concatenate(
            [
                jnp.concatenate([value[:side, :LANES], value[side:, :LANES]], axis=1),
                jnp.concatenate([value[:side, LANES:], value[side:, LANES:]], axis=1),
            ],
            axis=0,
        )

    def wave_of(member):
        angle, first, second, offset = place(member)
        pair, index, turn = source(angle, first, offset)
        unused_pair, next_index, next_turn = source(angle, second, offset)
        inner = lanes < LANES - offset

        def window(ref):
            return jnp.where(
                inner, pltpu.roll(ref[pair, index], turn, 1), pltpu.roll(ref[pair, next_index], next_turn, 1)
            )

        cosine, sine = window(cos_ref), window(sin_ref)
        probe_re, probe_im = probe_ref[0], probe_ref[1]
        return probe_re * cosine - probe_im * sine, probe_re * sine + probe_im * cosine

    def add(member, grad):
        angle, first, second, offset = place(member)
        turned = pltpu.roll(grad, offset, 1)
        kept = lanes >= offset
        acc[angle, first] += jnp.where(kept, turned, 0.0)
        acc[angle, second] += jnp.where(kept, 0.0, turned)

    def residual(far, two):
        far_re, far_im = far[:side], far[side:]
        amplitude = jnp.concatenate([measured_ref[member] for member in two], axis=1).astype(F32)
        factor = 1.0 - amplitude * lax.rsqrt(far_re * far_re + far_im * far_im + SMOOTHING)
        return jnp.concatenate([(far_re * factor).astype(BF16), (far_im * factor).astype(BF16)], axis=0)

    def step(number, carried):
        duos = [(number * GROUP + 2 * duo, number * GROUP + 2 * duo + 1) for duo in range(GROUP // 2)]
        waves = [[wave_of(member) for member in two] for two in duos]
        halves = []
        for both in waves:
            stacked = jnp.concatenate(
                [jnp.concatenate([re.astype(BF16), im.astype(BF16)], axis=1) for re, im in both], axis=0
            )
            halves.append(jnp.dot(stacked, minus_ref[...], preferred_element_type=F32).astype(BF16))
        fars = [jnp.dot(plus_ref[...], by_lane(half), preferred_element_type=F32) for half in halves]
        resids = [residual(far, two) for far, two in zip(fars, duos)]
        backs = [jnp.dot(minus_ref[...], resid, preferred_element_type=F32).astype(BF16) for resid in resids]
        nears = [jnp.dot(by_lane(back), plus_ref[...], preferred_element_type=F32) for back in backs]
        for near, two, both in zip(nears, duos, waves):
            for slot, member in enumerate(two):
                wave_re, wave_im = both[slot]
                cut = slice(slot * side, (slot + 1) * side)
                add(member, near[cut, LANES:] * wave_re - near[cut, :LANES] * wave_im)
        return carried

    lax.fori_loop(0, frames // GROUP, step, 0)
    for p in range(pairs):
        for hi in range(2):
            for b in range(own):
                out_ref[p, hi * own + b] = acc[p + hi * pairs, b].astype(WIRE)
        out_ref[p, 2 * own] = halo_join(acc[p, own], acc[p + pairs, own]).astype(WIRE)


def complex_tables(length):
    indices = np.arange(length)
    phases = (indices[:, None] * indices[None, :] % length) * (2.0 * math.pi / length)
    cosine, sine = np.cos(phases), np.sin(phases)
    minus = np.block([[cosine, -sine], [sine, cosine]])
    plus = np.block([[cosine, sine], [-sine, cosine]]) / length
    return jnp.asarray(minus, BF16), jnp.asarray(plus, BF16)


def frame_gradients(owner, shift, cosine, sine, probe, measured, own):
    pairs, pieces, rows, unused = cosine.shape
    smem = pl.BlockSpec(memory_space=pltpu.SMEM)
    vmem = pl.BlockSpec(memory_space=pltpu.VMEM)
    return pl.pallas_call(
        functools.partial(frame_kernel, own),
        out_shape=jax.ShapeDtypeStruct(cosine.shape, WIRE),
        in_specs=[smem, smem] + [vmem] * 6,
        out_specs=vmem,
        scratch_shapes=[pltpu.VMEM((2 * pairs, own + 1, rows, LANES), F32)],
        compiler_params=pltpu.CompilerParams(vmem_limit_bytes=48 * 1024 * 1024),
        name="frames",
    )(owner, shift, cosine, sine, probe, measured, *complex_tables(LANES))


def backproject_kernel(slices, blocks, lhs_ref, ker_ref, out_ref):
    half_rows = slices * blocks
    left = lane_ids((half_rows, LANES)) < HALF
    width = 8 * HALF
    start = pl.multiple_of(pl.program_id(0) * width, width)
    result = jnp.dot(lhs_ref[...], ker_ref[:, pl.ds(start, width)], preferred_element_type=F32)
    for pair in range(4):
        cols = slice(pair * LANES, (pair + 1) * LANES)
        lower, upper = result[:half_rows, cols], result[half_rows:, cols]
        crossed = pltpu.roll(jnp.where(left, upper, lower), HALF, 1)
        first = jnp.where(left, lower, crossed)
        second = jnp.where(left, crossed, upper)
        for s in range(slices):
            cut = slice(s * blocks, (s + 1) * blocks)
            out_ref[s, 0, pl.ds(2 * pair, blocks, stride=8), :] = first[cut]
            out_ref[s, 0, pl.ds(2 * pair + 1, blocks, stride=8), :] = second[cut]


def backproject(lhs, kernels, slices, beams, blocks):
    groups = beams // 8
    result = pl.pallas_call(
        functools.partial(backproject_kernel, slices, blocks),
        out_shape=jax.ShapeDtypeStruct((slices, groups, blocks * 8, LANES), F32),
        grid=(groups,),
        in_specs=[pl.BlockSpec(memory_space=pltpu.VMEM)] * 2,
        out_specs=pl.BlockSpec((slices, 1, blocks * 8, LANES), lambda g: (0, g, 0, 0)),
        compiler_params=pltpu.CompilerParams(vmem_limit_bytes=32 * 1024 * 1024),
        name="backproject",
    )(lhs, kernels)
    result = result.reshape(slices, groups, blocks, 8, LANES).transpose(0, 1, 3, 2, 4)
    return result.reshape(slices, beams, blocks * LANES)


def body(volume, shears, tile_shift, illumination, measured, frame_owner, frame_shift):
    tiles, slabs = lax.axis_size("tile"), lax.axis_size("slab")
    slices, beams, width = volume.shape
    blocks = width // LANES
    offsets = tile_shift.reshape(-1)
    owner = frame_owner.reshape(-1)
    cosine, sine = phase_waves(shears, offsets, volume, tiles, slabs)
    grads = frame_gradients(owner, frame_shift, cosine, sine, illumination, measured, blocks // tiles)
    lhs, kernels = back_operands(shears, offsets, grads, tiles, slabs, blocks, beams)
    return backproject(lhs, kernels, slices, beams, blocks)


def solution(mesh):
    in_specs = (
        P("slab", "tile", None),
        P(),
        P(None, "tile"),
        P(),
        P(("slab", "tile"), None, None),
        P(("slab", "tile"), None),
        P(("slab", "tile")),
    )
    out_specs = P("slab", "tile", None)
    return jax.shard_map(body, mesh=mesh, in_specs=in_specs, out_specs=out_specs, check_vma=False)
```

time: 72.7 us -> 55.3 us (0.76)
  Pallas kernels: 66.9 us -> 55 us
  local copies, waits for them, and re-layouts: 4.35 us -> 0.03 us
  other arithmetic: 1.1 us -> 0 us
    pallas_call x4 -> x3, Pallas kernels: 55.9 us -> 48.4 us  [the longest x1 24.3 us: phase_waves(): pl.pallas_call(functools.partial(phase_kernel, tiles, slabs, slices, beam...]
    pallas_call x1, Pallas kernels: 11.1 us -> 6.62 us  [frame_gradients(): pl.pallas_call(functools.partial(frame_kernel, own), out_shape=jax.ShapeD...]
    unnamed x14 -> x16, local copies, waits for them, and re-layouts: 4.35 us -> 0.03 us
where the time goes in v1:
time: 55.3 us; the launch traced here: 55.2 us
  Pallas kernels  55 us (99%)
    pallas_call x1, Pallas kernels, phase_waves(): pl.pallas_call(functools.partial(phase_kernel, tiles, slabs, slices, beam...  24.3 us
    pallas_call x1, Pallas kernels, back_operands(): pl.pallas_call(functools.partial(grad_kernel, tiles, slabs, blocks, beams...  18.1 us
    pallas_call x1, Pallas kernels, frame_gradients(): pl.pallas_call(functools.partial(frame_kernel, own), out_shape=jax.ShapeD...  6.62 us
    pallas_call x1, Pallas kernels, backproject(): pl.pallas_call(functools.partial(backproject_kernel, slices, blocks), out...  5.99 us

profile of v1, /device:TPU:0, one launch (start us, length us, event | category | flops | bytes accessed | tf_op | source)
XLA Modules:
  0.0 55.2 jit_solution(10934746330226634331)
XLA Ops:
  0.0 0.0 copy-start.2
  0.0 0.0 copy-start.3
  0.0 0.0 copy-start.7
  0.0 0.0 copy-start.6
  0.0 0.0 copy-start
  0.0 0.0 copy-start.1
  0.0 0.0 copy-start.4
  0.0 0.0 copy-start.5
  0.0 24.3 %phase_waves.1 = (f32[4,5,128,128]{3,2,1,0:T(8,128)S(1)}, f32[4,5,128,128]{3,2,1,0:T(8,128)S(1)}) custom-call(f32[8]{0:T(128)} %shears_ref.1, s32[8]{0:T(128)} %bitcast.12, f32[16,8,64,128]{3,2,1,0:T(8,128)} %bitcast.15), custom_call_target="tpu_custom_call" | custom-call | tf_op jit(solution)/shard_map/phase_waves/pallas_call | solution.py:232
  24.3 0.0 copy-done.2
  24.3 0.0 copy-done.3
  24.4 0.0 copy-done.7
  24.4 0.0 copy-done.6
  24.4 0.0 copy-done
  24.4 0.0 copy-done.1
  24.4 6.6 %frames.1.grad_ref = bf16[4,5,128,128]{3,2,1,0:T(8,128)(2,1)S(1)} custom-call(s32[32]{0:T(128)S(1)} %bitcast.14, s32[32]{0:T(128)S(1)} %copy-done.7, f32[4,5,128,128]{3,2,1,0:T(8,128)S(1)} %get-tuple-element.9.cos_ref, f32[4,5,128,128]{3,2,1,0:T(8,128)S(1)} %get-tuple-element.10.sin_ref, f32[2,128,128]{2,1,0:T(8,128)S(1)} %copy-done.1, ...), custom_call_target="tpu_custom_call" | custom-call | tf_op jit(solution)/shard_map/frames/pallas_call | solution.py:506
  31.0 0.0 copy-done.4
  31.0 0.0 copy-done.5
  31.0 18.1 %back_operands.1 = (bf16[256,1024]{1,0:T(8,128)(2,1)S(1)}, bf16[1024,4096]{1,0:T(8,128)(2,1)S(1)}) custom-call(f32[8]{0:T(128)S(1)} %copy-done.4, s32[8]{0:T(128)S(1)} %bitcast.13, bf16[4,5,128,128]{3,2,1,0:T(8,128)(2,1)S(1)} %frames.1.grad_ref), custom_call_target="tpu_custom_call" | custom-call | tf_op jit(solution)/shard_map/back_operands/pallas_call | solution.py:377
  49.2 6.0 %backproject.1 = f32[16,8,64,128]{3,2,1,0:T(8,128)} custom-call(bf16[256,1024]{1,0:T(8,128)(2,1)S(1)} %get-tuple-element.11.lhs_ref, bf16[1024,4096]{1,0:T(8,128)(2,1)S(1)} %get-tuple-element.12.ker_ref), custom_call_target="tpu_custom_call" | custom-call | tf_op jit(solution)/shard_map/backproject/pallas_call | solution.py:537
Async XLA Ops:
  0.0 24.3 %copy-start.2 = (bf16[256,256]{1,0:T(8,128)(2,1)S(1)}, bf16[256,256]{1,0:T(8,128)(2,1)}, u32[]{:S(2)}) copy-start(bf16[256,256]{1,0:T(8,128)(2,1)} %constant.5.clone.plus_ref) | copy-start | bytes 393220
  0.0 24.3 %copy-start.3 = (bf16[256,256]{1,0:T(8,128)(2,1)S(1)}, bf16[256,256]{1,0:T(8,128)(2,1)}, u32[]{:S(2)}) copy-start(bf16[256,256]{1,0:T(8,128)(2,1)} %constant.4.clone.minus_ref) | copy-start | bytes 393220
  0.0 24.4 %copy-start.7 = (s32[32]{0:T(128)S(1)}, s32[32]{0:T(128)}, u32[]{:S(2)}) copy-start(s32[32]{0:T(128)} %start_ref.1) | copy-start | bytes 388
  0.0 24.4 %copy-start.6 = (s32[32,1]{0,1:T(1,128)S(1)}, s32[32,1]{0,1:T(1,128)}, u32[]{:S(2)}) copy-start(s32[32,1]{0,1:T(1,128)} %param.14) | copy-start | bytes 388
  0.0 24.4 %copy-start = (bf16[32,128,128]{2,1,0:T(8,128)(2,1)S(1)}, bf16[32,128,128]{2,1,0:T(8,128)(2,1)}, u32[]{:S(2)}) copy-start(bf16[32,128,128]{2,1,0:T(8,128)(2,1)} %measured_ref.1) | copy-start | bytes 3145732
  0.0 24.4 %copy-start.1 = (f32[2,128,128]{2,1,0:T(8,128)S(1)}, f32[2,128,128]{2,1,0:T(8,128)}, u32[]{:S(2)}) copy-start(f32[2,128,128]{2,1,0:T(8,128)} %probe_ref.1) | copy-start | bytes 393220
  0.0 31.0 %copy-start.4 = (f32[8]{0:T(128)S(1)}, f32[8]{0:T(128)}, u32[]{:S(2)}) copy-start(f32[8]{0:T(128)} %shears_ref.1) | copy-start | bytes 100
  0.0 31.0 %copy-start.5 = (s32[8,1]{0,1:T(1,128)S(1)}, s32[8,1]{0,1:T(1,128)}, u32[]{:S(2)}) copy-start(s32[8,1]{0,1:T(1,128)} %param.11) | copy-start | bytes 100

commit v2 on v1

--- a/solution.py
+++ b/solution.py
@@ -18,7 +18,9 @@
 BF16 = jnp.bfloat16
 MESH = pl.DeviceIdType.MESH
 ROOT = math.sqrt(0.5 * math.log2(math.e))
-GROUP = 8
+GROUP = 32
+PHASE_CUTS = 4
+GRAD_CUTS = 4
 SIN_POLY = (3.1415926401307073, -5.1677100835078775, 2.550077523214199, -0.5982912856179897, 0.07765766030124945)
 COS_POLY = (0.9999999532476078, -4.934792830619626, 4.0584113528622625, -1.331876568078962, 0.2196896110945085)
 
@@ -48,6 +50,11 @@
             )
             total += 1
     return barrier, total
+
+
+def cuts_of(pairs, parts):
+    ends = [pairs * part // parts for part in range(parts + 1)]
+    return [(low, high) for low, high in zip(ends, ends[1:]) if low < high]
 
 
 def sin_cos(phase):
@@ -91,6 +98,8 @@
         volume_copy(group).start()
     barrier, greetings = signal_peers((("tile", tiles), ("slab", slabs)))
 
+    cuts = cuts_of(pairs, PHASE_CUTS)
+
     def tile_copy(p, step):
         peer = lax.rem(me_t + step, tiles)
         return pltpu.make_async_remote_copy(
@@ -102,17 +111,42 @@
             device_id_type=MESH,
         )
 
-    def slab_copy(p, step):
+    def slab_copy(c, step):
+        low, high = cuts[c]
         return pltpu.make_async_remote_copy(
-            src_ref=phase.at[p, :, rows, :],
-            dst_ref=phase.at[p, :, rows, :],
-            send_sem=slab_send.at[step - 1, p],
-            recv_sem=slab_recv.at[step - 1, p],
+            src_ref=phase.at[low:high, :, rows, :],
+            dst_ref=phase.at[low:high, :, rows, :],
+            send_sem=slab_send.at[step - 1, c],
+            recv_sem=slab_recv.at[step - 1, c],
             device_id={"slab": lax.rem(me_s + step, slabs)},
             device_id_type=MESH,
         )
 
+    shape = (HALF, LANES)
+    base = (lane_ids(shape) - row_ids(shape) - HALO).astype(F32) * ROOT
+    lanes = lane_ids((half_rows, LANES))
+    lanes_s = lane_ids((slices, LANES))
+    zero = jnp.zeros((slices, LANES), F32)
+
+    def make_beam_group(p, group):
+        steps = [shears_ref[p] * ROOT, shears_ref[p + pairs] * ROOT]
+        for beam in range(8):
+            q = group * 8 + beam
+            place = q.astype(F32) - (beams - 1) * 0.5
+            row = pl.multiple_of(q * HALF, HALF)
+            for side in range(2):
+                gap = base - place * steps[side]
+                ker[pl.ds(row, HALF), side * LANES : (side + 1) * LANES] = jnp.exp2(-(gap * gap)).astype(BF16)
+
+    def make_beams(p):
+        def group_step(group, carried):
+            make_beam_group(p, group)
+            return carried
+
+        lax.fori_loop(0, groups, group_step, 0)
+
     def arrange(group, carried):
+        make_beam_group(0, group)
         volume_copy(group).wait()
         for pair in range(4):
             col = pl.multiple_of((group * 4 + pair) * LANES, LANES)
@@ -131,25 +165,6 @@
                 lhs[row : row + 2 * blocks, pl.ds(col, LANES)] = jnp.concatenate(upper, 0).astype(BF16)
         return carried
 
-    shape = (HALF, LANES)
-    base = (lane_ids(shape) - row_ids(shape) - HALO).astype(F32) * ROOT
-    lanes = lane_ids((half_rows, LANES))
-    lanes_s = lane_ids((slices, LANES))
-    zero = jnp.zeros((slices, LANES), F32)
-
-    def make_beams(p):
-        steps = [shears_ref[p] * ROOT, shears_ref[p + pairs] * ROOT]
-
-        def beam(q, carried):
-            place = q.astype(F32) - (beams - 1) * 0.5
-            row = pl.multiple_of(q * HALF, HALF)
-            for side in range(2):
-                gap = base - place * steps[side]
-                ker[pl.ds(row, HALF), side * LANES : (side + 1) * LANES] = jnp.exp2(-(gap * gap)).astype(BF16)
-            return carried
-
-        lax.fori_loop(0, beams, beam, 0, unroll=8)
-
     def shifted_sums(p, side):
         cols = slice(side * LANES, (side + 1) * LANES)
         near = pltpu.roll(res[0:half_rows, cols], HALO, 1)
@@ -183,7 +198,6 @@
 
     for copy in small:
         copy.wait()
-    make_beams(0)
     lax.fori_loop(0, groups, arrange, 0)
     project_pair(0)
     pl.semaphore_wait(barrier, greetings)
@@ -193,30 +207,40 @@
             project_pair(p)
         for step in range(1, tiles):
             tile_copy(p, step).start()
+    for c, (low, high) in enumerate(cuts):
+        for p in range(low, high):
+            total = parts[me_t, p].astype(F32)
+            for step in range(1, tiles):
+                tile_copy(p, step).wait_recv()
+                total += came[step - 1, p].astype(F32)
+            phase[p, :, rows, :] = total.astype(WIRE)
+        for step in range(1, slabs):
+            slab_copy(c, step).start()
+    starts = {low: c for c, (low, high) in enumerate(cuts)}
     for p in range(pairs):
-        total = parts[me_t, p].astype(F32)
-        for step in range(1, tiles):
-            tile_copy(p, step).wait_recv()
-            total += came[step - 1, p].astype(F32)
-        phase[p, :, rows, :] = total.astype(WIRE)
-        for step in range(1, slabs):
-            slab_copy(p, step).start()
-    for p in range(pairs):
-        for step in range(1, slabs):
-            slab_copy(p, step).wait_recv()
+        if p in starts:
+            for step in range(1, slabs):
+                slab_copy(starts[p], step).wait_recv()
 
         def wave_piece(piece, carried):
             sine, cosine = sin_cos(phase[p, piece].astype(F32))
-            sin_ref[p, piece] = sine
-            cos_ref[p, piece] = cosine
+            place = piece + jnp.where(piece >= own, 1, 0)
+            sin_ref[p, place] = sine
+            cos_ref[p, place] = cosine
             return carried
 
-        lax.fori_loop(0, phase.shape[1], wave_piece, 0)
+        lax.fori_loop(0, 2 * own, wave_piece, 0)
+        sine, cosine = sin_cos(phase[p, 2 * own].astype(F32))
+        sin_ref[p, own] = sine
+        cos_ref[p, own] = cosine
+        sin_ref[p, 2 * own + 1] = pltpu.roll(sine, HALF, 1)
+        cos_ref[p, 2 * own + 1] = pltpu.roll(cosine, HALF, 1)
     for p in range(pairs):
         for step in range(1, tiles):
             tile_copy(p, step).wait_send()
+    for c in range(len(cuts)):
         for step in range(1, slabs):
-            slab_copy(p, step).wait_send()
+            slab_copy(c, step).wait_send()
 
 
 def phase_waves(shears, tile_shift, volume, tiles, slabs):
@@ -228,7 +252,7 @@
     view = volume.reshape(slices, groups, 8, blocks, LANES).transpose(0, 1, 3, 2, 4)
     view = view.reshape(slices, groups, blocks * 8, LANES)
     rows = 2 * slices * blocks
-    waves = jax.ShapeDtypeStruct((pairs, pieces, slabs * slices, LANES), F32)
+    waves = jax.ShapeDtypeStruct((pairs, 2 * (own + 1), slabs * slices, LANES), F32)
     return pl.pallas_call(
         functools.partial(phase_kernel, tiles, slabs, slices, beams, blocks),
         out_shape=(waves, waves),
@@ -275,67 +299,80 @@
     me_t = lax.axis_index("tile")
     me_s = lax.axis_index("slab")
     barrier, greetings = signal_peers((("tile", tiles), ("slab", slabs)))
-    pl.semaphore_wait(barrier, greetings)
 
     def rows_of(slab):
         return pl.ds(pl.multiple_of(slab * slices, slices), slices)
 
-    def slab_copy(p, step):
+    cuts = cuts_of(pairs, GRAD_CUTS)
+
+    def slab_copy(c, step):
         peer = lax.rem(me_s + step, slabs)
+        low, high = cuts[c]
         return pltpu.make_async_remote_copy(
-            src_ref=grad_ref.at[p, :, rows_of(peer), :],
-            dst_ref=came.at[step - 1, p],
-            send_sem=slab_send.at[step - 1, p],
-            recv_sem=slab_recv.at[step - 1, p],
+            src_ref=grad_ref.at[low:high, :, rows_of(peer), :],
+            dst_ref=came.at[step - 1, low:high],
+            send_sem=slab_send.at[step - 1, c],
+            recv_sem=slab_recv.at[step - 1, c],
             device_id={"slab": peer},
             device_id_type=MESH,
         )
 
-    def tile_copy(p, step):
+    def tile_copy(c, step):
+        low, high = cuts[c]
         return pltpu.make_async_remote_copy(
-            src_ref=gathered.at[me_t, p],
-            dst_ref=gathered.at[me_t, p],
-            send_sem=tile_send.at[step - 1, p],
-            recv_sem=tile_recv.at[step - 1, p],
+            src_ref=gathered.at[me_t, low:high],
+            dst_ref=gathered.at[me_t, low:high],
+            send_sem=tile_send.at[step - 1, c],
+            recv_sem=tile_recv.at[step - 1, c],
             device_id={"tile": lax.rem(me_t + step, tiles)},
             device_id_type=MESH,
         )
 
-    for p in range(pairs):
-        for step in range(1, slabs):
-            slab_copy(p, step).start()
-
     shape = (LANES, LANES)
     base = (row_ids(shape) - lane_ids(shape) % HALF - HALO).astype(F32) * ROOT
     pick = (lane_ids((1, LANES)) >= HALF).astype(F32) - (beams - 1) * 0.5
-    for a in range(2 * pairs):
-        slope = shears_ref[a] * ROOT
-
-        def beam(pair, carried):
-            gap = base - (pick + (2 * pair).astype(F32)) * slope
-            col = pl.multiple_of(pair * LANES, LANES)
-            ker_ref[a * LANES : (a + 1) * LANES, pl.ds(col, LANES)] = jnp.exp2(-(gap * gap)).astype(BF16)
-            return carried
-
-        lax.fori_loop(0, beams // 2, beam, 0, unroll=8)
-
-    for p in range(pairs):
-        total = grad_ref[p, :, rows_of(me_s), :].astype(F32)
+
+    def make_beams(angles):
+        for a in angles:
+            slope = shears_ref[a] * ROOT
+
+            def beam(pair, carried):
+                gap = base - (pick + (2 * pair).astype(F32)) * slope
+                col = pl.multiple_of(pair * LANES, LANES)
+                ker_ref[a * LANES : (a + 1) * LANES, pl.ds(col, LANES)] = jnp.exp2(-(gap * gap)).astype(BF16)
+                return carried
+
+            lax.fori_loop(0, beams // 2, beam, 0, unroll=8)
+
+    early = pairs // 2
+    make_beams(range(early))
+    pl.semaphore_wait(barrier, greetings)
+    for c in range(len(cuts)):
         for step in range(1, slabs):
-            slab_copy(p, step).wait_recv()
-            total += came[step - 1, p].astype(F32)
-        gathered[me_t, p] = total.astype(WIRE)
+            slab_copy(c, step).start()
+    make_beams(range(early, 2 * pairs))
+
+    for c, (low, high) in enumerate(cuts):
+        for step in range(1, slabs):
+            slab_copy(c, step).wait_recv()
+        for p in range(low, high):
+            total = grad_ref[p, :, rows_of(me_s), :].astype(F32)
+            for step in range(1, slabs):
+                total += came[step - 1, p].astype(F32)
+            gathered[me_t, p] = total.astype(WIRE)
         for step in range(1, tiles):
-            tile_copy(p, step).start()
+            tile_copy(c, step).start()
 
     lanes = lane_ids((slices, LANES))
     zero = jnp.zeros((slices, LANES), F32)
     for edge in (0, blocks + 1, blocks + 2):
         near[edge] = zero
         far[edge] = zero
+    starts = {low: c for c, (low, high) in enumerate(cuts)}
     for p in range(pairs):
-        for step in range(1, tiles):
-            tile_copy(p, step).wait_recv()
+        if p in starts:
+            for step in range(1, tiles):
+                tile_copy(starts[p], step).wait_recv()
         for hi in range(2):
             a = p + hi * pairs
             margins = []
@@ -360,11 +397,11 @@
                 rows_f32[pl.ds(i, slices, stride=blocks), :] = lower
                 rows_f32[pl.ds(half_rows + i, slices, stride=blocks), :] = upper
             lhs_ref[:, a * LANES : (a + 1) * LANES] = rows_f32[...].astype(BF16)
-    for p in range(pairs):
+    for c in range(len(cuts)):
         for step in range(1, tiles):
-            tile_copy(p, step).wait_send()
+            tile_copy(c, step).wait_send()
         for step in range(1, slabs):
-            slab_copy(p, step).wait_send()
+            slab_copy(c, step).wait_send()
 
 
 def back_operands(shears, tile_shift, grads, tiles, slabs, blocks, beams):
@@ -418,13 +455,6 @@
         second = jnp.where(first + 1 == ring, 0, first + 1)
         return angle, first, second, offset
 
-    def source(angle, block, offset):
-        upper = jnp.where(angle >= pairs, 1, 0)
-        margin = block == own
-        index = jnp.where(margin, 2 * own, upper * own + block)
-        turn = jnp.where(margin, upper * HALF, 0) + LANES - offset
-        return angle - upper * pairs, index, jnp.where(turn >= LANES, turn - LANES, turn)
-
     def by_lane(value):
         return jnp.concatenate(
             [
@@ -436,14 +466,13 @@
 
     def wave_of(member):
         angle, first, second, offset = place(member)
-        pair, index, turn = source(angle, first, offset)
-        unused_pair, next_index, next_turn = source(angle, second, offset)
-        inner = lanes < LANES - offset
+        upper = jnp.where(angle >= pairs, 1, 0)
+        pair = angle - upper * pairs
+        outer = lanes >= offset
+        turn = jnp.where(offset > 0, LANES - offset, 0)
 
         def window(ref):
-            return jnp.where(
-                inner, pltpu.roll(ref[pair, index], turn, 1), pltpu.roll(ref[pair, next_index], next_turn, 1)
-            )
+            return pltpu.roll(jnp.where(outer, ref[pair, upper * ring + first], ref[pair, upper * ring + second]), turn, 1)
 
         cosine, sine = window(cos_ref), window(sin_ref)
         probe_re, probe_im = probe_ref[0], probe_ref[1]
@@ -500,12 +529,12 @@
 
 
 def frame_gradients(owner, shift, cosine, sine, probe, measured, own):
-    pairs, pieces, rows, unused = cosine.shape
+    pairs, waves, rows, unused = cosine.shape
     smem = pl.BlockSpec(memory_space=pltpu.SMEM)
     vmem = pl.BlockSpec(memory_space=pltpu.VMEM)
     return pl.pallas_call(
         functools.partial(frame_kernel, own),
-        out_shape=jax.ShapeDtypeStruct(cosine.shape, WIRE),
+        out_shape=jax.ShapeDtypeStruct((pairs, waves - 1, rows, LANES), WIRE),
         in_specs=[smem, smem] + [vmem] * 6,
         out_specs=vmem,
         scratch_shapes=[pltpu.VMEM((2 * pairs, own + 1, rows, LANES), F32)],
@@ -514,32 +543,49 @@
     )(owner, shift, cosine, sine, probe, measured, *complex_tables(LANES))
 
 
-def backproject_kernel(slices, blocks, lhs_ref, ker_ref, out_ref):
+def backproject_kernel(slices, blocks, beams, lhs_ref, ker_ref, out_hbm, out_ref, sems):
+    groups = beams // 8
+    width = 8 * HALF
     half_rows = slices * blocks
     left = lane_ids((half_rows, LANES)) < HALF
-    width = 8 * HALF
-    start = pl.multiple_of(pl.program_id(0) * width, width)
-    result = jnp.dot(lhs_ref[...], ker_ref[:, pl.ds(start, width)], preferred_element_type=F32)
-    for pair in range(4):
-        cols = slice(pair * LANES, (pair + 1) * LANES)
-        lower, upper = result[:half_rows, cols], result[half_rows:, cols]
-        crossed = pltpu.roll(jnp.where(left, upper, lower), HALF, 1)
-        first = jnp.where(left, lower, crossed)
-        second = jnp.where(left, crossed, upper)
-        for s in range(slices):
-            cut = slice(s * blocks, (s + 1) * blocks)
-            out_ref[s, 0, pl.ds(2 * pair, blocks, stride=8), :] = first[cut]
-            out_ref[s, 0, pl.ds(2 * pair + 1, blocks, stride=8), :] = second[cut]
+
+    def copy_out(group):
+        return pltpu.make_async_copy(out_ref.at[:, group], out_hbm.at[:, group], sems.at[group])
+
+    def step(group, carried):
+        start = pl.multiple_of(group * width, width)
+        result = jnp.dot(lhs_ref[...], ker_ref[:, pl.ds(start, width)], preferred_element_type=F32)
+        for pair in range(4):
+            cols = slice(pair * LANES, (pair + 1) * LANES)
+            lower, upper = result[:half_rows, cols], result[half_rows:, cols]
+            crossed = pltpu.roll(jnp.where(left, upper, lower), HALF, 1)
+            first = jnp.where(left, lower, crossed)
+            second = jnp.where(left, crossed, upper)
+            for s in range(slices):
+                cut = slice(s * blocks, (s + 1) * blocks)
+                out_ref[s, group, pl.ds(2 * pair, blocks, stride=8), :] = first[cut]
+                out_ref[s, group, pl.ds(2 * pair + 1, blocks, stride=8), :] = second[cut]
+        copy_out(group).start()
+        return carried
+
+    lax.fori_loop(0, groups, step, 0, unroll=True)
+
+    def finish(group, carried):
+        copy_out(group).wait()
+        return carried
+
+    lax.fori_loop(0, groups, finish, 0)
 
 
 def backproject(lhs, kernels, slices, beams, blocks):
     groups = beams // 8
+    shape = (slices, groups, blocks * 8, LANES)
     result = pl.pallas_call(
-        functools.partial(backproject_kernel, slices, blocks),
-        out_shape=jax.ShapeDtypeStruct((slices, groups, blocks * 8, LANES), F32),
-        grid=(groups,),
+        functools.partial(backproject_kernel, slices, blocks, beams),
+        out_shape=jax.ShapeDtypeStruct(shape, F32),
         in_specs=[pl.BlockSpec(memory_space=pltpu.VMEM)] * 2,
-        out_specs=pl.BlockSpec((slices, 1, blocks * 8, LANES), lambda g: (0, g, 0, 0)),
+        out_specs=pl.BlockSpec(memory_space=pltpu.HBM),
+        scratch_shapes=[pltpu.VMEM(shape, F32), pltpu.SemaphoreType.DMA((groups,))],
         compiler_params=pltpu.CompilerParams(vmem_limit_bytes=32 * 1024 * 1024),
         name="backproject",
     )(lhs, kernels)

time: 55.3 us -> 51.3 us (0.928)
  Pallas kernels: 55 us -> 50.9 us
    pallas_call x1, Pallas kernels: 5.99 us -> 3.57 us  [backproject(): pl.pallas_call(functools.partial(backproject_kernel, slices, blocks, beam...]
    pallas_call x1, Pallas kernels: 6.62 us -> 4.67 us  [frame_gradients(): pl.pallas_call(functools.partial(frame_kernel, own), out_shape=jax.ShapeD...]
where the time goes in v2:
time: 51.3 us; the launch traced here: 51.2 us
  Pallas kernels  50.9 us (99%)
    pallas_call x1, Pallas kernels, phase_waves(): pl.pallas_call(functools.partial(phase_kernel, tiles, slabs, slices, beam...  24.7 us
    pallas_call x1, Pallas kernels, back_operands(): pl.pallas_call(functools.partial(grad_kernel, tiles, slabs, blocks, beams...  17.9 us
    pallas_call x1, Pallas kernels, frame_gradients(): pl.pallas_call(functools.partial(frame_kernel, own), out_shape=jax.ShapeD...  4.67 us
    pallas_call x1, Pallas kernels, backproject(): pl.pallas_call(functools.partial(backproject_kernel, slices, blocks, beam...  3.57 us

profile of v2, /device:TPU:0, one launch (start us, length us, event | category | flops | bytes accessed | tf_op | source)
XLA Modules:
  0.0 51.2 jit_solution(16152390820078106745)
XLA Ops:
  0.0 0.0 copy-start.2
  0.0 0.0 copy-start.3
  0.0 0.0 copy-start.7
  0.0 0.0 copy-start.6
  0.0 0.0 copy-start
  0.0 0.0 copy-start.1
  0.0 0.0 copy-start.4
  0.0 0.0 copy-start.5
  0.0 24.7 %phase_waves.1 = (f32[4,6,128,128]{3,2,1,0:T(8,128)S(1)}, f32[4,6,128,128]{3,2,1,0:T(8,128)S(1)}) custom-call(f32[8]{0:T(128)} %shears_ref.1, s32[8]{0:T(128)} %bitcast.12, f32[16,8,64,128]{3,2,1,0:T(8,128)} %bitcast.15), custom_call_target="tpu_custom_call" | custom-call | tf_op jit(solution)/shard_map/phase_waves/pallas_call | solution.py:256
  24.8 0.0 copy-done.2
  24.8 0.0 copy-done.3
  24.8 0.0 copy-done.7
  24.8 0.0 copy-done.6
  24.8 0.0 copy-done
  24.8 0.0 copy-done.1
  24.8 4.7 %frames.1.grad_ref = bf16[4,5,128,128]{3,2,1,0:T(8,128)(2,1)S(1)} custom-call(s32[32]{0:T(128)S(1)} %bitcast.14, s32[32]{0:T(128)S(1)} %copy-done.7, f32[4,6,128,128]{3,2,1,0:T(8,128)S(1)} %get-tuple-element.9.cos_ref, f32[4,6,128,128]{3,2,1,0:T(8,128)S(1)} %get-tuple-element.10.sin_ref, f32[2,128,128]{2,1,0:T(8,128)S(1)} %copy-done.1, ...), custom_call_target="tpu_custom_call" | custom-call | tf_op jit(solution)/shard_map/frames/pallas_call | solution.py:535
  29.5 0.0 copy-done.4
  29.5 0.0 copy-done.5
  29.5 17.9 %back_operands.1 = (bf16[256,1024]{1,0:T(8,128)(2,1)S(1)}, bf16[1024,4096]{1,0:T(8,128)(2,1)S(1)}) custom-call(f32[8]{0:T(128)S(1)} %copy-done.4, s32[8]{0:T(128)S(1)} %bitcast.13, bf16[4,5,128,128]{3,2,1,0:T(8,128)(2,1)S(1)} %frames.1.grad_ref), custom_call_target="tpu_custom_call" | custom-call | tf_op jit(solution)/shard_map/back_operands/pallas_call | solution.py:414
  47.4 3.6 %backproject.1 = f32[16,8,64,128]{3,2,1,0:T(8,128)} custom-call(bf16[256,1024]{1,0:T(8,128)(2,1)S(1)} %get-tuple-element.11.lhs_ref, bf16[1024,4096]{1,0:T(8,128)(2,1)S(1)} %get-tuple-element.12.ker_ref), custom_call_target="tpu_custom_call" | custom-call | tf_op jit(solution)/shard_map/backproject/pallas_call | solution.py:583
Async XLA Ops:
  0.0 24.8 %copy-start.2 = (bf16[256,256]{1,0:T(8,128)(2,1)S(1)}, bf16[256,256]{1,0:T(8,128)(2,1)}, u32[]{:S(2)}) copy-start(bf16[256,256]{1,0:T(8,128)(2,1)} %constant.5.clone.plus_ref) | copy-start | bytes 393220
  0.0 24.8 %copy-start.3 = (bf16[256,256]{1,0:T(8,128)(2,1)S(1)}, bf16[256,256]{1,0:T(8,128)(2,1)}, u32[]{:S(2)}) copy-start(bf16[256,256]{1,0:T(8,128)(2,1)} %constant.4.clone.minus_ref) | copy-start | bytes 393220
  0.0 24.8 %copy-start.7 = (s32[32]{0:T(128)S(1)}, s32[32]{0:T(128)}, u32[]{:S(2)}) copy-start(s32[32]{0:T(128)} %start_ref.1) | copy-start | bytes 388
  0.0 24.8 %copy-start.6 = (s32[32,1]{0,1:T(1,128)S(1)}, s32[32,1]{0,1:T(1,128)}, u32[]{:S(2)}) copy-start(s32[32,1]{0,1:T(1,128)} %param.14) | copy-start | bytes 388
  0.0 24.8 %copy-start = (bf16[32,128,128]{2,1,0:T(8,128)(2,1)S(1)}, bf16[32,128,128]{2,1,0:T(8,128)(2,1)}, u32[]{:S(2)}) copy-start(bf16[32,128,128]{2,1,0:T(8,128)(2,1)} %measured_ref.1) | copy-start | bytes 3145732
  0.0 24.8 %copy-start.1 = (f32[2,128,128]{2,1,0:T(8,128)S(1)}, f32[2,128,128]{2,1,0:T(8,128)}, u32[]{:S(2)}) copy-start(f32[2,128,128]{2,1,0:T(8,128)} %probe_ref.1) | copy-start | bytes 393220
  0.0 29.5 %copy-start.4 = (f32[8]{0:T(128)S(1)}, f32[8]{0:T(128)}, u32[]{:S(2)}) copy-start(f32[8]{0:T(128)} %shears_ref.1) | copy-start | bytes 100
  0.0 29.5 %copy-start.5 = (s32[8,1]{0,1:T(1,128)S(1)}, s32[8,1]{0,1:T(1,128)}, u32[]{:S(2)}) copy-start(s32[8,1]{0,1:T(1,128)} %param.11) | copy-start | bytes 100

commit v3 on v2

--- a/solution.py
+++ b/solution.py
@@ -122,7 +122,7 @@
             device_id_type=MESH,
         )
 
-    shape = (HALF, LANES)
+    shape = (16, LANES)
     base = (lane_ids(shape) - row_ids(shape) - HALO).astype(F32) * ROOT
     lanes = lane_ids((half_rows, LANES))
     lanes_s = lane_ids((slices, LANES))
@@ -132,21 +132,20 @@
         steps = [shears_ref[p] * ROOT, shears_ref[p + pairs] * ROOT]
         for beam in range(8):
             q = group * 8 + beam
-            place = q.astype(F32) - (beams - 1) * 0.5
-            row = pl.multiple_of(q * HALF, HALF)
+            place = jnp.asarray(q, F32) - (beams - 1) * 0.5
+            row = q * HALF if isinstance(q, int) else pl.multiple_of(q * HALF, HALF)
             for side in range(2):
                 gap = base - place * steps[side]
-                ker[pl.ds(row, HALF), side * LANES : (side + 1) * LANES] = jnp.exp2(-(gap * gap)).astype(BF16)
+                rows_of = jnp.exp2(-(gap * gap)).astype(BF16)
+                for turn in range(HALF // 16):
+                    turned = pltpu.roll(rows_of, 16 * turn, 1) if turn else rows_of
+                    ker[p % 2, pl.ds(row + 16 * turn, 16), side * LANES : (side + 1) * LANES] = turned
 
     def make_beams(p):
-        def group_step(group, carried):
+        for group in range(groups):
             make_beam_group(p, group)
-            return carried
-
-        lax.fori_loop(0, groups, group_step, 0)
 
     def arrange(group, carried):
-        make_beam_group(0, group)
         volume_copy(group).wait()
         for pair in range(4):
             col = pl.multiple_of((group * 4 + pair) * LANES, LANES)
@@ -184,7 +183,9 @@
         return row_of
 
     def project_pair(p):
-        res[...] = jnp.dot(lhs[...], ker[...], preferred_element_type=F32)
+        if p:
+            make_beams(p)
+        res[...] = jnp.dot(lhs[...], ker[p % 2], preferred_element_type=F32)
         sums = [shifted_sums(p, side) for side in range(2)]
         for t in range(tiles):
             margins = []
@@ -198,12 +199,12 @@
 
     for copy in small:
         copy.wait()
+    make_beams(0)
     lax.fori_loop(0, groups, arrange, 0)
     project_pair(0)
     pl.semaphore_wait(barrier, greetings)
     for p in range(pairs):
         if p:
-            make_beams(p)
             project_pair(p)
         for step in range(1, tiles):
             tile_copy(p, step).start()
@@ -263,7 +264,7 @@
             pltpu.SMEM((angles,), jnp.int32),
             pltpu.VMEM((groups, slices, blocks * 8, LANES), F32),
             pltpu.VMEM((rows, beams * HALF), BF16),
-            pltpu.VMEM((beams * HALF, 2 * LANES), BF16),
+            pltpu.VMEM((2, beams * HALF, 2 * LANES), BF16),
             pltpu.VMEM((rows, 2 * LANES), F32),
             pltpu.VMEM((2, 2, rows // 2, LANES), F32),
             pltpu.VMEM((tiles, pairs, pieces, slices, LANES), WIRE),

time: 51.3 us -> 47.8 us (0.932)
  Pallas kernels: 50.9 us -> 47.4 us
    pallas_call x1, Pallas kernels: 24.7 us -> 21.6 us  [phase_waves(): pl.pallas_call(functools.partial(phase_kernel, tiles, slabs, slices, beam...]
where the time goes in v3:
time: 47.8 us; the launch traced here: 47.7 us
  Pallas kernels  47.4 us (99%)
    pallas_call x1, Pallas kernels, phase_waves(): pl.pallas_call(functools.partial(phase_kernel, tiles, slabs, slices, beam...  21.6 us
    pallas_call x1, Pallas kernels, back_operands(): pl.pallas_call(functools.partial(grad_kernel, tiles, slabs, blocks, beams...  17.5 us
    pallas_call x1, Pallas kernels, frame_gradients(): pl.pallas_call(functools.partial(frame_kernel, own), out_shape=jax.ShapeD...  4.67 us
    pallas_call x1, Pallas kernels, backproject(): pl.pallas_call(functools.partial(backproject_kernel, slices, blocks, beam...  3.57 us

profile of v3, /device:TPU:0, one launch (start us, length us, event | category | flops | bytes accessed | tf_op | source)
XLA Modules:
  0.0 47.7 jit_solution(6001695013029525133)
XLA Ops:
  0.0 0.0 copy-start.2
  0.0 0.0 copy-start.3
  0.0 0.0 copy-start.7
  0.0 0.0 copy-start.6
  0.0 0.0 copy-start
  0.0 0.0 copy-start.1
  0.0 0.0 copy-start.4
  0.0 0.0 copy-start.5
  0.0 21.6 %phase_waves.1 = (f32[4,6,128,128]{3,2,1,0:T(8,128)S(1)}, f32[4,6,128,128]{3,2,1,0:T(8,128)S(1)}) custom-call(f32[8]{0:T(128)} %shears_ref.1, s32[8]{0:T(128)} %bitcast.12, f32[16,8,64,128]{3,2,1,0:T(8,128)} %bitcast.15), custom_call_target="tpu_custom_call" | custom-call | tf_op jit(solution)/shard_map/phase_waves/pallas_call | solution.py:257
  21.7 0.0 copy-done.2
  21.7 0.0 copy-done.3
  21.7 0.0 copy-done.7
  21.7 0.0 copy-done.6
  21.7 0.0 copy-done
  21.7 0.0 copy-done.1
  21.7 4.7 %frames.1.grad_ref = bf16[4,5,128,128]{3,2,1,0:T(8,128)(2,1)S(1)} custom-call(s32[32]{0:T(128)S(1)} %bitcast.14, s32[32]{0:T(128)S(1)} %copy-done.7, f32[4,6,128,128]{3,2,1,0:T(8,128)S(1)} %get-tuple-element.9.cos_ref, f32[4,6,128,128]{3,2,1,0:T(8,128)S(1)} %get-tuple-element.10.sin_ref, f32[2,128,128]{2,1,0:T(8,128)S(1)} %copy-done.1, ...), custom_call_target="tpu_custom_call" | custom-call | tf_op jit(solution)/shard_map/frames/pallas_call | solution.py:536
  26.4 0.0 copy-done.4
  26.4 0.0 copy-done.5
  26.4 17.5 %back_operands.1 = (bf16[256,1024]{1,0:T(8,128)(2,1)S(1)}, bf16[1024,4096]{1,0:T(8,128)(2,1)S(1)}) custom-call(f32[8]{0:T(128)S(1)} %copy-done.4, s32[8]{0:T(128)S(1)} %bitcast.13, bf16[4,5,128,128]{3,2,1,0:T(8,128)(2,1)S(1)} %frames.1.grad_ref), custom_call_target="tpu_custom_call" | custom-call | tf_op jit(solution)/shard_map/back_operands/pallas_call | solution.py:415
  44.0 3.6 %backproject.1 = f32[16,8,64,128]{3,2,1,0:T(8,128)} custom-call(bf16[256,1024]{1,0:T(8,128)(2,1)S(1)} %get-tuple-element.11.lhs_ref, bf16[1024,4096]{1,0:T(8,128)(2,1)S(1)} %get-tuple-element.12.ker_ref), custom_call_target="tpu_custom_call" | custom-call | tf_op jit(solution)/shard_map/backproject/pallas_call | solution.py:584
Async XLA Ops:
  0.0 21.7 %copy-start.2 = (bf16[256,256]{1,0:T(8,128)(2,1)S(1)}, bf16[256,256]{1,0:T(8,128)(2,1)}, u32[]{:S(2)}) copy-start(bf16[256,256]{1,0:T(8,128)(2,1)} %constant.5.clone.plus_ref) | copy-start | bytes 393220
  0.0 21.7 %copy-start.3 = (bf16[256,256]{1,0:T(8,128)(2,1)S(1)}, bf16[256,256]{1,0:T(8,128)(2,1)}, u32[]{:S(2)}) copy-start(bf16[256,256]{1,0:T(8,128)(2,1)} %constant.4.clone.minus_ref) | copy-start | bytes 393220
  0.0 21.7 %copy-start.7 = (s32[32]{0:T(128)S(1)}, s32[32]{0:T(128)}, u32[]{:S(2)}) copy-start(s32[32]{0:T(128)} %start_ref.1) | copy-start | bytes 388
  0.0 21.7 %copy-start.6 = (s32[32,1]{0,1:T(1,128)S(1)}, s32[32,1]{0,1:T(1,128)}, u32[]{:S(2)}) copy-start(s32[32,1]{0,1:T(1,128)} %param.14) | copy-start | bytes 388
  0.0 21.7 %copy-start = (bf16[32,128,128]{2,1,0:T(8,128)(2,1)S(1)}, bf16[32,128,128]{2,1,0:T(8,128)(2,1)}, u32[]{:S(2)}) copy-start(bf16[32,128,128]{2,1,0:T(8,128)(2,1)} %measured_ref.1) | copy-start | bytes 3145732
  0.0 21.7 %copy-start.1 = (f32[2,128,128]{2,1,0:T(8,128)S(1)}, f32[2,128,128]{2,1,0:T(8,128)}, u32[]{:S(2)}) copy-start(f32[2,128,128]{2,1,0:T(8,128)} %probe_ref.1) | copy-start | bytes 393220
  0.0 26.4 %copy-start.4 = (f32[8]{0:T(128)S(1)}, f32[8]{0:T(128)}, u32[]{:S(2)}) copy-start(f32[8]{0:T(128)} %shears_ref.1) | copy-start | bytes 100
  0.0 26.4 %copy-start.5 = (s32[8,1]{0,1:T(1,128)S(1)}, s32[8,1]{0,1:T(1,128)}, u32[]{:S(2)}) copy-start(s32[8,1]{0,1:T(1,128)} %param.11) | copy-start | bytes 100

commit v4 on v3

--- a/solution.py
+++ b/solution.py
@@ -20,7 +20,6 @@
 ROOT = math.sqrt(0.5 * math.log2(math.e))
 GROUP = 32
 PHASE_CUTS = 4
-GRAD_CUTS = 4
 SIN_POLY = (3.1415926401307073, -5.1677100835078775, 2.550077523214199, -0.5982912856179897, 0.07765766030124945)
 COS_POLY = (0.9999999532476078, -4.934792830619626, 4.0584113528622625, -1.331876568078962, 0.2196896110945085)
 
@@ -290,41 +289,51 @@
 
 def grad_kernel(
     tiles, slabs, blocks, beams,
-    shears_ref, shift_ref, grad_ref, lhs_ref, ker_ref,
-    gathered, near, far, rows_f32, came, slab_send, slab_recv, tile_send, tile_recv,
+    shears_ref, shift_ref, grad_ref, lhs_ref, ker_ref, part_ref,
+    core_came, pair_sum, came, gathered, near, far, rows_f32, old_lhs, old_ker,
+    core_send, core_recv, slab_send, slab_recv, tile_send, tile_recv,
 ):
-    pairs, pieces = grad_ref.shape[:2]
+    pairs, pieces, chips, both_rows = grad_ref.shape[:4]
     own = (pieces - 1) // 2
-    slices = gathered.shape[3]
+    slices = both_rows // 2
     half_rows = slices * blocks
+    last = pairs - 1
     me_t = lax.axis_index("tile")
     me_s = lax.axis_index("slab")
+    me_chip = me_s // 2
+    me_core = me_s - 2 * me_chip
     barrier, greetings = signal_peers((("tile", tiles), ("slab", slabs)))
 
-    def rows_of(slab):
-        return pl.ds(pl.multiple_of(slab * slices, slices), slices)
-
-    cuts = cuts_of(pairs, GRAD_CUTS)
-
-    def slab_copy(c, step):
-        peer = lax.rem(me_s + step, slabs)
-        low, high = cuts[c]
+    def rows_of(core):
+        return pl.ds(pl.multiple_of(core * slices, slices), slices)
+
+    def core_copy(p):
         return pltpu.make_async_remote_copy(
-            src_ref=grad_ref.at[low:high, :, rows_of(peer), :],
-            dst_ref=came.at[step - 1, low:high],
-            send_sem=slab_send.at[step - 1, c],
-            recv_sem=slab_recv.at[step - 1, c],
-            device_id={"slab": peer},
+            src_ref=grad_ref.at[p, :, :, rows_of(1 - me_core), :],
+            dst_ref=core_came.at[p],
+            send_sem=core_send.at[p],
+            recv_sem=core_recv.at[p],
+            device_id={"slab": 2 * me_chip + 1 - me_core},
             device_id_type=MESH,
         )
 
-    def tile_copy(c, step):
-        low, high = cuts[c]
+    def slab_copy(p, step):
+        peer = lax.rem(me_chip + step, chips)
         return pltpu.make_async_remote_copy(
-            src_ref=gathered.at[me_t, low:high],
-            dst_ref=gathered.at[me_t, low:high],
-            send_sem=tile_send.at[step - 1, c],
-            recv_sem=tile_recv.at[step - 1, c],
+            src_ref=pair_sum.at[p, :, peer],
+            dst_ref=came.at[step - 1, p],
+            send_sem=slab_send.at[step - 1, p],
+            recv_sem=slab_recv.at[step - 1, p],
+            device_id={"slab": 2 * peer + me_core},
+            device_id_type=MESH,
+        )
+
+    def tile_copy(p, step):
+        return pltpu.make_async_remote_copy(
+            src_ref=gathered.at[me_t, p],
+            dst_ref=gathered.at[me_t, p],
+            send_sem=tile_send.at[step - 1, p],
+            recv_sem=tile_recv.at[step - 1, p],
             device_id={"tile": lax.rem(me_t + step, tiles)},
             device_id_type=MESH,
         )
@@ -333,49 +342,50 @@
     base = (row_ids(shape) - lane_ids(shape) % HALF - HALO).astype(F32) * ROOT
     pick = (lane_ids((1, LANES)) >= HALF).astype(F32) - (beams - 1) * 0.5
 
-    def make_beams(angles):
-        for a in angles:
-            slope = shears_ref[a] * ROOT
+    def make_beams(p):
+        for hi in range(2):
+            slope = shears_ref[p + hi * pairs] * ROOT
+            target, row = (ker_ref, hi * LANES) if p == last else (old_ker, (2 * p + hi) * LANES)
 
             def beam(pair, carried):
                 gap = base - (pick + (2 * pair).astype(F32)) * slope
                 col = pl.multiple_of(pair * LANES, LANES)
-                ker_ref[a * LANES : (a + 1) * LANES, pl.ds(col, LANES)] = jnp.exp2(-(gap * gap)).astype(BF16)
+                target[row : row + LANES, pl.ds(col, LANES)] = jnp.exp2(-(gap * gap)).astype(BF16)
                 return carried
 
             lax.fori_loop(0, beams // 2, beam, 0, unroll=8)
 
-    early = pairs // 2
-    make_beams(range(early))
+    make_beams(0)
     pl.semaphore_wait(barrier, greetings)
-    for c in range(len(cuts)):
-        for step in range(1, slabs):
-            slab_copy(c, step).start()
-    make_beams(range(early, 2 * pairs))
-
-    for c, (low, high) in enumerate(cuts):
-        for step in range(1, slabs):
-            slab_copy(c, step).wait_recv()
-        for p in range(low, high):
-            total = grad_ref[p, :, rows_of(me_s), :].astype(F32)
-            for step in range(1, slabs):
-                total += came[step - 1, p].astype(F32)
-            gathered[me_t, p] = total.astype(WIRE)
+    for p in range(pairs):
+        core_copy(p).start()
+    for p in range(pairs):
+        core_copy(p).wait_recv()
+        mine = grad_ref[p, :, :, rows_of(me_core), :].astype(F32)
+        pair_sum[p] = (mine + core_came[p].astype(F32)).astype(WIRE)
+        for step in range(1, chips):
+            slab_copy(p, step).start()
+    if pairs > 1:
+        make_beams(1)
+    for p in range(pairs):
+        total = pair_sum[p, :, me_chip].astype(F32)
+        for step in range(1, chips):
+            slab_copy(p, step).wait_recv()
+            total += came[step - 1, p].astype(F32)
+        gathered[me_t, p] = total.astype(WIRE)
         for step in range(1, tiles):
-            tile_copy(c, step).start()
+            tile_copy(p, step).start()
+    if pairs > 2:
+        make_beams(2)
 
     lanes = lane_ids((slices, LANES))
     zero = jnp.zeros((slices, LANES), F32)
     for edge in (0, blocks + 1, blocks + 2):
         near[edge] = zero
         far[edge] = zero
-    starts = {low: c for c, (low, high) in enumerate(cuts)}
-    for p in range(pairs):
-        if p in starts:
-            for step in range(1, tiles):
-                tile_copy(starts[p], step).wait_recv()
+
+    def left_operand(p):
         for hi in range(2):
-            a = p + hi * pairs
             margins = []
             for t in range(tiles):
                 margin = gathered[t, p, 2 * own].astype(F32)
@@ -390,44 +400,76 @@
                     k = t * own + b + 1
                     near[k] = pltpu.roll(value, LANES - HALO, 1)
                     far[k] = pltpu.roll(value, LANES - HALO - HALF, 1)
-            shift = shift_ref[a]
+            shift = shift_ref[p + hi * pairs]
             for i in range(blocks):
                 k = i + 1 + shift
                 lower = jnp.where(lanes < LANES - HALO, near[k], near[k + 1])
                 upper = jnp.where(lanes < LANES - HALO - HALF, far[k], far[k + 1])
                 rows_f32[pl.ds(i, slices, stride=blocks), :] = lower
                 rows_f32[pl.ds(half_rows + i, slices, stride=blocks), :] = upper
-            lhs_ref[:, a * LANES : (a + 1) * LANES] = rows_f32[...].astype(BF16)
-    for c in range(len(cuts)):
+            target, col = (lhs_ref, hi * LANES) if p == last else (old_lhs, (2 * p + hi) * LANES)
+            target[:, col : col + LANES] = rows_f32[...].astype(BF16)
+
+    def product(low, high):
+        depth = slice(2 * low * LANES, 2 * high * LANES)
+        width = 8 * HALF
+        for group in range(beams // 8):
+            span = slice(group * width, (group + 1) * width)
+            update = jnp.dot(old_lhs[:, depth], old_ker[depth, span], preferred_element_type=F32)
+            if low == 0:
+                part_ref[:, span] = update
+            else:
+                part_ref[:, span] += update
+
+    early = max(1, last - 1)
+    for p in range(pairs):
         for step in range(1, tiles):
-            tile_copy(c, step).wait_send()
-        for step in range(1, slabs):
-            slab_copy(c, step).wait_send()
+            tile_copy(p, step).wait_recv()
+        left_operand(p)
+        if p + 3 < pairs:
+            make_beams(p + 3)
+        if p == early - 1:
+            product(0, early)
+        elif early <= p < last:
+            product(p, p + 1)
+    for p in range(pairs):
+        core_copy(p).wait_send()
+        for step in range(1, tiles):
+            tile_copy(p, step).wait_send()
+        for step in range(1, chips):
+            slab_copy(p, step).wait_send()
 
 
 def back_operands(shears, tile_shift, grads, tiles, slabs, blocks, beams):
-    pairs, pieces, all_rows = grads.shape[:3]
-    slices = all_rows // slabs
-    angles = 2 * pairs
+    pairs, pieces, chips, both_rows = grads.shape[:4]
+    slices = both_rows // 2
     rows = 2 * slices * blocks
+    older = 2 * (pairs - 1) * LANES
     smem = pl.BlockSpec(memory_space=pltpu.SMEM)
     vmem = pl.BlockSpec(memory_space=pltpu.VMEM)
     return pl.pallas_call(
         functools.partial(grad_kernel, tiles, slabs, blocks, beams),
         out_shape=(
-            jax.ShapeDtypeStruct((rows, angles * LANES), BF16),
-            jax.ShapeDtypeStruct((angles * LANES, beams * HALF), BF16),
+            jax.ShapeDtypeStruct((rows, 2 * LANES), BF16),
+            jax.ShapeDtypeStruct((2 * LANES, beams * HALF), BF16),
+            jax.ShapeDtypeStruct((rows, beams * HALF), F32),
         ),
         in_specs=[smem, smem, vmem],
-        out_specs=(vmem, vmem),
+        out_specs=(vmem, vmem, vmem),
         scratch_shapes=[
+            pltpu.VMEM((pairs, pieces, chips, slices, LANES), WIRE),
+            pltpu.VMEM((pairs, pieces, chips, slices, LANES), WIRE),
+            pltpu.VMEM((chips - 1, pairs, pieces, slices, LANES), WIRE),
             pltpu.VMEM((tiles, pairs, pieces, slices, LANES), WIRE),
             pltpu.VMEM((blocks + 3, slices, LANES), F32),
             pltpu.VMEM((blocks + 3, slices, LANES), F32),
             pltpu.VMEM((rows, LANES), F32),
-            pltpu.VMEM((slabs - 1, pairs, pieces, slices, LANES), WIRE),
-            pltpu.SemaphoreType.DMA((slabs - 1, pairs)),
-            pltpu.SemaphoreType.DMA((slabs - 1, pairs)),
+            pltpu.VMEM((rows, older), BF16),
+            pltpu.VMEM((older, beams * HALF), BF16),
+            pltpu.SemaphoreType.DMA((pairs,)),
+            pltpu.SemaphoreType.DMA((pairs,)),
+            pltpu.SemaphoreType.DMA((chips - 1, pairs)),
+            pltpu.SemaphoreType.DMA((chips - 1, pairs)),
             pltpu.SemaphoreType.DMA((tiles - 1, pairs)),
             pltpu.SemaphoreType.DMA((tiles - 1, pairs)),
         ],
@@ -516,8 +558,8 @@
     for p in range(pairs):
         for hi in range(2):
             for b in range(own):
-                out_ref[p, hi * own + b] = acc[p + hi * pairs, b].astype(WIRE)
-        out_ref[p, 2 * own] = halo_join(acc[p, own], acc[p + pairs, own]).astype(WIRE)
+                out_ref[p, hi * own + b] = acc[p + hi * pairs, b].astype(WIRE).reshape(out_ref.shape[2:])
+        out_ref[p, 2 * own] = halo_join(acc[p, own], acc[p + pairs, own]).astype(WIRE).reshape(out_ref.shape[2:])
 
 
 def complex_tables(length):
@@ -529,13 +571,13 @@
     return jnp.asarray(minus, BF16), jnp.asarray(plus, BF16)
 
 
-def frame_gradients(owner, shift, cosine, sine, probe, measured, own):
+def frame_gradients(owner, shift, cosine, sine, probe, measured, own, chips):
     pairs, waves, rows, unused = cosine.shape
     smem = pl.BlockSpec(memory_space=pltpu.SMEM)
     vmem = pl.BlockSpec(memory_space=pltpu.VMEM)
     return pl.pallas_call(
         functools.partial(frame_kernel, own),
-        out_shape=jax.ShapeDtypeStruct((pairs, waves - 1, rows, LANES), WIRE),
+        out_shape=jax.ShapeDtypeStruct((pairs, waves - 1, chips, rows // chips, LANES), WIRE),
         in_specs=[smem, smem] + [vmem] * 6,
         out_specs=vmem,
         scratch_shapes=[pltpu.VMEM((2 * pairs, own + 1, rows, LANES), F32)],
@@ -544,7 +586,7 @@
     )(owner, shift, cosine, sine, probe, measured, *complex_tables(LANES))
 
 
-def backproject_kernel(slices, blocks, beams, lhs_ref, ker_ref, out_hbm, out_ref, sems):
+def backproject_kernel(slices, blocks, beams, lhs_ref, ker_ref, part_ref, out_hbm, out_ref, sems):
     groups = beams // 8
     width = 8 * HALF
     half_rows = slices * blocks
@@ -555,7 +597,8 @@
 
     def step(group, carried):
         start = pl.multiple_of(group * width, width)
-        result = jnp.dot(lhs_ref[...], ker_ref[:, pl.ds(start, width)], preferred_element_type=F32)
+        span = pl.ds(start, width)
+        result = part_ref[:, span] + jnp.dot(lhs_ref[...], ker_ref[:, span], preferred_element_type=F32)
         for pair in range(4):
             cols = slice(pair * LANES, (pair + 1) * LANES)
             lower, upper = result[:half_rows, cols], result[half_rows:, cols]
@@ -578,18 +621,18 @@
     lax.fori_loop(0, groups, finish, 0)
 
 
-def backproject(lhs, kernels, slices, beams, blocks):
+def backproject(lhs, kernels, partial_sum, slices, beams, blocks):
     groups = beams // 8
     shape = (slices, groups, blocks * 8, LANES)
     result = pl.pallas_call(
         functools.partial(backproject_kernel, slices, blocks, beams),
         out_shape=jax.ShapeDtypeStruct(shape, F32),
-        in_specs=[pl.BlockSpec(memory_space=pltpu.VMEM)] * 2,
+        in_specs=[pl.BlockSpec(memory_space=pltpu.VMEM)] * 3,
         out_specs=pl.BlockSpec(memory_space=pltpu.HBM),
         scratch_shapes=[pltpu.VMEM(shape, F32), pltpu.SemaphoreType.DMA((groups,))],
         compiler_params=pltpu.CompilerParams(vmem_limit_bytes=32 * 1024 * 1024),
         name="backproject",
-    )(lhs, kernels)
+    )(lhs, kernels, partial_sum)
     result = result.reshape(slices, groups, blocks, 8, LANES).transpose(0, 1, 3, 2, 4)
     return result.reshape(slices, beams, blocks * LANES)
 
@@ -601,9 +644,9 @@
     offsets = tile_shift.reshape(-1)
     owner = frame_owner.reshape(-1)
     cosine, sine = phase_waves(shears, offsets, volume, tiles, slabs)
-    grads = frame_gradients(owner, frame_shift, cosine, sine, illumination, measured, blocks // tiles)
-    lhs, kernels = back_operands(shears, offsets, grads, tiles, slabs, blocks, beams)
-    return backproject(lhs, kernels, slices, beams, blocks)
+    grads = frame_gradients(owner, frame_shift, cosine, sine, illumination, measured, blocks // tiles, slabs // 2)
+    lhs, kernels, partial_sum = back_operands(shears, offsets, grads, tiles, slabs, blocks, beams)
+    return backproject(lhs, kernels, partial_sum, slices, beams, blocks)
 
 
 def solution(mesh):

time: 47.8 us -> 46.7 us (0.977)
  Pallas kernels: 47.4 us -> 46.2 us
    pallas_call x1, Pallas kernels: 3.57 us -> 2.51 us  [backproject(): pl.pallas_call(functools.partial(backproject_kernel, slices, blocks, beam...]
where the time goes in v4:
time: 46.7 us; the launch traced here: 46.5 us
  Pallas kernels  46.2 us (99%)
    pallas_call x1, Pallas kernels, phase_waves(): pl.pallas_call(functools.partial(phase_kernel, tiles, slabs, slices, beam...  21.6 us
    pallas_call x1, Pallas kernels, back_operands(): pl.pallas_call(functools.partial(grad_kernel, tiles, slabs, blocks, beams...  17.4 us
    pallas_call x1, Pallas kernels, frame_gradients(): pl.pallas_call(functools.partial(frame_kernel, own), out_shape=jax.ShapeD...  4.67 us
    pallas_call x1, Pallas kernels, backproject(): pl.pallas_call(functools.partial(backproject_kernel, slices, blocks, beam...  2.51 us

profile of v4, /device:TPU:0, one launch (start us, length us, event | category | flops | bytes accessed | tf_op | source)
XLA Modules:
  0.0 46.5 jit_solution(15574299485096525135)
XLA Ops:
  0.0 0.0 copy-start.2
  0.0 0.0 copy-start.3
  0.0 0.0 copy-start.7
  0.0 0.0 copy-start.6
  0.0 0.0 copy-start
  0.0 0.0 copy-start.1
  0.0 0.0 copy-start.4
  0.0 0.0 copy-start.5
  0.0 21.6 %phase_waves.1 = (f32[4,6,128,128]{3,2,1,0:T(8,128)S(1)}, f32[4,6,128,128]{3,2,1,0:T(8,128)S(1)}) custom-call(f32[8]{0:T(128)} %shears_ref.1, s32[8]{0:T(128)} %bitcast.12, f32[16,8,64,128]{3,2,1,0:T(8,128)} %bitcast.15), custom_call_target="tpu_custom_call" | custom-call | tf_op jit(solution)/shard_map/phase_waves/pallas_call | solution.py:256
  21.7 0.0 copy-done.2
  21.7 0.0 copy-done.3
  21.7 0.0 copy-done.7
  21.7 0.0 copy-done.6
  21.7 0.0 copy-done
  21.7 0.0 copy-done.1
  21.7 4.7 %frames.1.grad_ref = bf16[4,5,4,32,128]{4,3,2,1,0:T(8,128)(2,1)S(1)} custom-call(s32[32]{0:T(128)S(1)} %bitcast.14, s32[32]{0:T(128)S(1)} %copy-done.7, f32[4,6,128,128]{3,2,1,0:T(8,128)S(1)} %get-tuple-element.10.cos_ref, f32[4,6,128,128]{3,2,1,0:T(8,128)S(1)} %get-tuple-element.11.sin_ref, f32[2,128,128]{2,1,0:T(8,128)S(1)} %copy-done.1, ...), custom_call_target="tpu_custom_call" | custom-call | tf_op jit(solution)/shard_map/frames/pallas_call | solution.py:578
  26.4 0.0 copy-done.4
  26.4 0.0 copy-done.5
  26.4 17.4 %back_operands.1 = (bf16[256,256]{1,0:T(8,128)(2,1)S(1)}, bf16[256,4096]{1,0:T(8,128)(2,1)S(1)}, f32[256,4096]{1,0:T(8,128)S(1)}) custom-call(f32[8]{0:T(128)S(1)} %copy-done.4, s32[8]{0:T(128)S(1)} %bitcast.13, bf16[4,5,4,32,128]{4,3,2,1,0:T(8,128)(2,1)S(1)} %frames.1.grad_ref), custom_call_target="tpu_custom_call" | custom-call | tf_op jit(solution)/shard_map/back_operands/pallas_call | solution.py:450
  43.9 2.5 %backproject.1 = f32[16,8,64,128]{3,2,1,0:T(8,128)} custom-call(bf16[256,256]{1,0:T(8,128)(2,1)S(1)} %get-tuple-element.12.lhs_ref, bf16[256,4096]{1,0:T(8,128)(2,1)S(1)} %get-tuple-element.13.ker_ref, f32[256,4096]{1,0:T(8,128)S(1)} %get-tuple-element.14.part_ref), custom_call_target="tpu_custom_call" | custom-call | tf_op jit(solution)/shard_map/backproject/pallas_call | solution.py:627
Async XLA Ops:
  0.0 21.7 %copy-start.2 = (bf16[256,256]{1,0:T(8,128)(2,1)S(1)}, bf16[256,256]{1,0:T(8,128)(2,1)}, u32[]{:S(2)}) copy-start(bf16[256,256]{1,0:T(8,128)(2,1)} %constant.5.clone.plus_ref) | copy-start | bytes 393220
  0.0 21.7 %copy-start.3 = (bf16[256,256]{1,0:T(8,128)(2,1)S(1)}, bf16[256,256]{1,0:T(8,128)(2,1)}, u32[]{:S(2)}) copy-start(bf16[256,256]{1,0:T(8,128)(2,1)} %constant.4.clone.minus_ref) | copy-start | bytes 393220
  0.0 21.7 %copy-start.7 = (s32[32]{0:T(128)S(1)}, s32[32]{0:T(128)}, u32[]{:S(2)}) copy-start(s32[32]{0:T(128)} %start_ref.1) | copy-start | bytes 388
  0.0 21.7 %copy-start.6 = (s32[32,1]{0,1:T(1,128)S(1)}, s32[32,1]{0,1:T(1,128)}, u32[]{:S(2)}) copy-start(s32[32,1]{0,1:T(1,128)} %param.14) | copy-start | bytes 388
  0.0 21.7 %copy-start = (bf16[32,128,128]{2,1,0:T(8,128)(2,1)S(1)}, bf16[32,128,128]{2,1,0:T(8,128)(2,1)}, u32[]{:S(2)}) copy-start(bf16[32,128,128]{2,1,0:T(8,128)(2,1)} %measured_ref.1) | copy-start | bytes 3145732
  0.0 21.7 %copy-start.1 = (f32[2,128,128]{2,1,0:T(8,128)S(1)}, f32[2,128,128]{2,1,0:T(8,128)}, u32[]{:S(2)}) copy-start(f32[2,128,128]{2,1,0:T(8,128)} %probe_ref.1) | copy-start | bytes 393220
  0.0 26.4 %copy-start.4 = (f32[8]{0:T(128)S(1)}, f32[8]{0:T(128)}, u32[]{:S(2)}) copy-start(f32[8]{0:T(128)} %shears_ref.1) | copy-start | bytes 100
  0.0 26.4 %copy-start.5 = (s32[8,1]{0,1:T(1,128)S(1)}, s32[8,1]{0,1:T(1,128)}, u32[]{:S(2)}) copy-start(s32[8,1]{0,1:T(1,128)} %param.11) | copy-start | bytes 100

commit v5 on v4

--- a/solution.py
+++ b/solution.py
@@ -144,10 +144,10 @@
         for group in range(groups):
             make_beam_group(p, group)
 
-    def arrange(group, carried):
+    def arrange(group):
         volume_copy(group).wait()
         for pair in range(4):
-            col = pl.multiple_of((group * 4 + pair) * LANES, LANES)
+            col = (group * 4 + pair) * LANES
             for duo in range(slices // 2):
                 lower, upper = [], []
                 for s in (2 * duo, 2 * duo + 1):
@@ -158,10 +158,9 @@
                     lower.append(jnp.where(left, first, crossed))
                     upper.append(jnp.where(left, crossed, second))
                 row = 2 * duo * blocks
-                lhs[row : row + 2 * blocks, pl.ds(col, LANES)] = jnp.concatenate(lower, 0).astype(BF16)
+                lhs[row : row + 2 * blocks, col : col + LANES] = jnp.concatenate(lower, 0).astype(BF16)
                 row += half_rows
-                lhs[row : row + 2 * blocks, pl.ds(col, LANES)] = jnp.concatenate(upper, 0).astype(BF16)
-        return carried
+                lhs[row : row + 2 * blocks, col : col + LANES] = jnp.concatenate(upper, 0).astype(BF16)
 
     def shifted_sums(p, side):
         cols = slice(side * LANES, (side + 1) * LANES)
@@ -199,7 +198,8 @@
     for copy in small:
         copy.wait()
     make_beams(0)
-    lax.fori_loop(0, groups, arrange, 0)
+    for group in range(groups):
+        arrange(group)
     project_pair(0)
     pl.semaphore_wait(barrier, greetings)
     for p in range(pairs):

time: 46.7 us -> 46.5 us (level)
  no operation moved by 1% of the time
where the time goes in v5:
time: 46.5 us; the launch traced here: 46.4 us
  Pallas kernels  46 us (99%)
    pallas_call x1, Pallas kernels, phase_waves(): pl.pallas_call(functools.partial(phase_kernel, tiles, slabs, slices, beam...  21.5 us
    pallas_call x1, Pallas kernels, back_operands(): pl.pallas_call(functools.partial(grad_kernel, tiles, slabs, blocks, beams...  17.4 us
    pallas_call x1, Pallas kernels, frame_gradients(): pl.pallas_call(functools.partial(frame_kernel, own), out_shape=jax.ShapeD...  4.67 us
    pallas_call x1, Pallas kernels, backproject(): pl.pallas_call(functools.partial(backproject_kernel, slices, blocks, beam...  2.51 us

profile of v5, /device:TPU:0, one launch (start us, length us, event | category | flops | bytes accessed | tf_op | source)
XLA Modules:
  0.0 46.4 jit_solution(8608408043405785966)
XLA Ops:
  0.0 0.0 copy-start.2
  0.0 0.0 copy-start.3
  0.0 0.0 copy-start.7
  0.0 0.0 copy-start.6
  0.0 0.0 copy-start
  0.0 0.0 copy-start.1
  0.0 0.0 copy-start.4
  0.0 0.0 copy-start.5
  0.0 21.5 %phase_waves.1 = (f32[4,6,128,128]{3,2,1,0:T(8,128)S(1)}, f32[4,6,128,128]{3,2,1,0:T(8,128)S(1)}) custom-call(f32[8]{0:T(128)} %shears_ref.1, s32[8]{0:T(128)} %bitcast.12, f32[16,8,64,128]{3,2,1,0:T(8,128)} %bitcast.15), custom_call_target="tpu_custom_call" | custom-call | tf_op jit(solution)/shard_map/phase_waves/pallas_call | solution.py:256
  21.5 0.0 copy-done.2
  21.5 0.0 copy-done.3
  21.5 0.0 copy-done.7
  21.6 0.0 copy-done.6
  21.6 0.0 copy-done
  21.6 0.0 copy-done.1
  21.6 4.7 %frames.1.grad_ref = bf16[4,5,4,32,128]{4,3,2,1,0:T(8,128)(2,1)S(1)} custom-call(s32[32]{0:T(128)S(1)} %bitcast.14, s32[32]{0:T(128)S(1)} %copy-done.7, f32[4,6,128,128]{3,2,1,0:T(8,128)S(1)} %get-tuple-element.10.cos_ref, f32[4,6,128,128]{3,2,1,0:T(8,128)S(1)} %get-tuple-element.11.sin_ref, f32[2,128,128]{2,1,0:T(8,128)S(1)} %copy-done.1, ...), custom_call_target="tpu_custom_call" | custom-call | tf_op jit(solution)/shard_map/frames/pallas_call | solution.py:578
  26.3 0.0 copy-done.4
  26.3 0.0 copy-done.5
  26.3 17.4 %back_operands.1 = (bf16[256,256]{1,0:T(8,128)(2,1)S(1)}, bf16[256,4096]{1,0:T(8,128)(2,1)S(1)}, f32[256,4096]{1,0:T(8,128)S(1)}) custom-call(f32[8]{0:T(128)S(1)} %copy-done.4, s32[8]{0:T(128)S(1)} %bitcast.13, bf16[4,5,4,32,128]{4,3,2,1,0:T(8,128)(2,1)S(1)} %frames.1.grad_ref), custom_call_target="tpu_custom_call" | custom-call | tf_op jit(solution)/shard_map/back_operands/pallas_call | solution.py:450
  43.7 2.5 %backproject.1 = f32[16,8,64,128]{3,2,1,0:T(8,128)} custom-call(bf16[256,256]{1,0:T(8,128)(2,1)S(1)} %get-tuple-element.12.lhs_ref, bf16[256,4096]{1,0:T(8,128)(2,1)S(1)} %get-tuple-element.13.ker_ref, f32[256,4096]{1,0:T(8,128)S(1)} %get-tuple-element.14.part_ref), custom_call_target="tpu_custom_call" | custom-call | tf_op jit(solution)/shard_map/backproject/pallas_call | solution.py:627
Async XLA Ops:
  0.0 21.5 %copy-start.2 = (bf16[256,256]{1,0:T(8,128)(2,1)S(1)}, bf16[256,256]{1,0:T(8,128)(2,1)}, u32[]{:S(2)}) copy-start(bf16[256,256]{1,0:T(8,128)(2,1)} %constant.5.clone.plus_ref) | copy-start | bytes 393220
  0.0 21.5 %copy-start.3 = (bf16[256,256]{1,0:T(8,128)(2,1)S(1)}, bf16[256,256]{1,0:T(8,128)(2,1)}, u32[]{:S(2)}) copy-start(bf16[256,256]{1,0:T(8,128)(2,1)} %constant.4.clone.minus_ref) | copy-start | bytes 393220
  0.0 21.5 %copy-start.7 = (s32[32]{0:T(128)S(1)}, s32[32]{0:T(128)}, u32[]{:S(2)}) copy-start(s32[32]{0:T(128)} %start_ref.1) | copy-start | bytes 388
  0.0 21.6 %copy-start.6 = (s32[32,1]{0,1:T(1,128)S(1)}, s32[32,1]{0,1:T(1,128)}, u32[]{:S(2)}) copy-start(s32[32,1]{0,1:T(1,128)} %param.14) | copy-start | bytes 388
  0.0 21.6 %copy-start = (bf16[32,128,128]{2,1,0:T(8,128)(2,1)S(1)}, bf16[32,128,128]{2,1,0:T(8,128)(2,1)}, u32[]{:S(2)}) copy-start(bf16[32,128,128]{2,1,0:T(8,128)(2,1)} %measured_ref.1) | copy-start | bytes 3145732
  0.0 21.6 %copy-start.1 = (f32[2,128,128]{2,1,0:T(8,128)S(1)}, f32[2,128,128]{2,1,0:T(8,128)}, u32[]{:S(2)}) copy-start(f32[2,128,128]{2,1,0:T(8,128)} %probe_ref.1) | copy-start | bytes 393220
  0.0 26.2 %copy-start.4 = (f32[8]{0:T(128)S(1)}, f32[8]{0:T(128)}, u32[]{:S(2)}) copy-start(f32[8]{0:T(128)} %shears_ref.1) | copy-start | bytes 100
  0.0 26.2 %copy-start.5 = (s32[8,1]{0,1:T(1,128)S(1)}, s32[8,1]{0,1:T(1,128)}, u32[]{:S(2)}) copy-start(s32[8,1]{0,1:T(1,128)} %param.11) | copy-start | bytes 100
